TPU v7x, 512 devices: a whole 4x8x8 slice. The times are simulated.
512 devices in a mesh: ens: 16 (over x, y_hi), lat: 16 (over y_lo, z), lon: 2 (over core).
Axes of the slice: x: 4, y: 8 (y_hi: 4, y_lo: 2; y = y_hi * 2 + y_lo), z: 8, core: 2. Of those that a mesh axis runs over, the one named last changes fastest.
Arguments:
- hidden_state: bfloat16 [16, 90, 32, 720], P('ens', None, 'lat', 'lon'), may hold values from -6 to 6
- filter_coefficients: bfloat16 [9, 10, 90], replicated, may hold values from -0.21875 to 0.21875
- meridian_offset_table: int32 [3, 32], P(None, 'lat'), may hold values from 1 to 4
- function_pick_table: int32 [9, 32, 1440], P(None, 'lat', 'lon'), may hold values from 0 to 8
- observation: float32 [10, 32, 1440], P(None, 'lat', 'lon'), may hold values from -6 to 6
- latitude_cosine_factor: float32 [32], P('lat'), may hold values from 0.3 to 3
Outputs:
- latent_grad: float32 [16, 90, 32, 720], P('ens', None, 'lat', 'lon')
All inputs are finite; a program needn't handle non-finite values.
Results may differ from a plain program's by a relative error of at most 0.0037.
Values may be sent and summed in bfloat16 or wider, within the bound.
A program may use at most 64 MiB of HBM per device.

v0:
```python
import jax
import jax.numpy as jnp
from jax import lax
from jax.sharding import PartitionSpec as P

SPAN = 4


smooth_square = 0.01


def from_behind(block, axis, distance):
    devices = range(lax.axis_size(axis))
    route = [((i - distance) % len(devices), i) for i in devices]
    return lax.ppermute(block, axis, route)


def shifted(array, axis, by):
    count = lax.axis_size(axis)
    pairs = [(i, i + by) for i in range(count) if 0 <= i + by < count]
    return lax.ppermute(array, axis, pairs)


def padded(block, sides, width, periodic):
    for axis, dim in sides:
        count = lax.axis_size(axis)
        forward = [(i, i + 1) for i in range(count - 1)]
        if periodic:
            forward.append((count - 1, 0))
        backward = [(target, source) for source, target in forward]
        low = lax.ppermute(
            lax.slice_in_dim(block, block.shape[dim] - width, None, axis=dim), axis, forward
        )
        high = lax.ppermute(lax.slice_in_dim(block, 0, width, axis=dim), axis, backward)
        block = jnp.concatenate([low, block, high], axis=dim)
    return block


def laid_out(parts, dim):
    parts = jnp.moveaxis(parts, 0, dim)
    dims = parts.shape
    return parts.reshape(*dims[:dim], dims[dim] * dims[dim + 1], *dims[dim + 2 :])


def from_everyone(array, axis):
    count = lax.axis_size(axis)
    return lax.all_to_all(
        jnp.broadcast_to(array[None], (count, *array.shape)), axis, 0, 0, tiled=True
    )


def gathered_copies(array, axis, dim):
    return laid_out(from_everyone(array, axis), dim)


def smoothed_derivative(difference):
    return difference / jnp.sqrt(difference * difference + smooth_square)


def lon_send(piece, direction):
    return from_behind(piece, "lon", direction)


def lat_send(piece, direction):
    return shifted(piece, "lat", direction)


def on_device(
    hidden_state,
    filter_coefficients,
    meridian_offset_table,
    function_pick_table,
    observation,
    latitude_cosine_factor,
):
    basis_count, variables, channels = filter_coefficients.shape
    parallel_number = hidden_state.shape[2]
    latent_cols = hidden_state.shape[3]
    margin = SPAN // 2 + 1
    grid_cols = 2 * latent_cols
    extended_width = grid_cols + 2 * SPAN
    banded = padded(hidden_state[0], (("lat", 1),), 1, False)
    wrapped = padded(banded, (("lon", 2),), margin, True)
    latent_f32 = wrapped.astype(jnp.float32)
    halfway = 0.5 * (latent_f32[..., :-1] + latent_f32[..., 1:])
    refined = jnp.stack([latent_f32[..., :-1], halfway], axis=-1).reshape(
        channels, parallel_number + 2, -1
    )
    offset = 2 * margin - SPAN
    interpolated = refined[..., offset : offset + extended_width].astype(jnp.bfloat16)
    flat_weight = filter_coefficients.reshape(basis_count * variables, channels)
    product = jnp.dot(
        flat_weight, interpolated.reshape(channels, -1), preferred_element_type=jnp.float32
    )
    product = product.reshape(basis_count, variables, parallel_number + 2, extended_width)
    levels = jnp.arange(basis_count, dtype=jnp.int32)
    prediction = jnp.zeros((variables, parallel_number, grid_cols), jnp.float32)
    function_pick_filters = []
    for row_step in (-1, 0, 1):
        band_rows = product[:, :, 1 + row_step : 1 + row_step + parallel_number, :]
        row_stride = meridian_offset_table[row_step + 1][:, None]
        for col_step in (-1, 0, 1):
            adjacent_position = 3 * (row_step + 1) + col_step + 1
            if col_step == 0:
                picked = band_rows[..., SPAN : SPAN + grid_cols]
            else:
                begin = SPAN + col_step
                picked = band_rows[..., begin : begin + grid_cols]
                for stride_value in range(2, SPAN + 1):
                    begin = SPAN + col_step * stride_value
                    picked = jnp.where(
                        row_stride == stride_value,
                        band_rows[..., begin : begin + grid_cols],
                        picked,
                    )
            picked_function = (
                function_pick_table[adjacent_position][None] == levels[:, None, None]
            ).astype(jnp.float32)
            function_pick_filters.append(picked_function)
            prediction = prediction + jnp.sum(picked_function[:, None] * picked, axis=0)
    points = parallel_number * grid_cols
    own_values = prediction.reshape(1, variables, points)
    sample_number = lax.axis_size("ens")
    pair_total = jnp.sum(
        smoothed_derivative(own_values - gathered_copies(own_values, "ens", 0)), axis=0
    )
    pair_total = pair_total.reshape(variables, parallel_number, grid_cols)
    prediction_derivative = latitude_cosine_factor[None, :, None] * (
        smoothed_derivative(prediction - observation) - pair_total / (sample_number - 1)
    )
    product_grad = jnp.zeros(
        (basis_count, variables, parallel_number + 2, extended_width), jnp.float32
    )
    for row_step in (-1, 0, 1):
        row_stride = meridian_offset_table[row_step + 1][None, None, :, None]
        collected = jnp.zeros(
            (basis_count, variables, parallel_number, extended_width), jnp.float32
        )
        for col_step in (-1, 0, 1):
            adjacent_position = 3 * (row_step + 1) + col_step + 1
            sample_dispersion = (
                function_pick_filters[adjacent_position][:, None] * prediction_derivative[None]
            )
            if col_step == 0:
                collected = collected + jnp.pad(
                    sample_dispersion, ((0, 0), (0, 0), (0, 0), (SPAN, SPAN))
                )
            else:
                for stride_value in range(1, SPAN + 1):
                    begin = SPAN + col_step * stride_value
                    masked = jnp.where(row_stride == stride_value, sample_dispersion, 0.0)
                    collected = collected + jnp.pad(
                        masked, ((0, 0), (0, 0), (0, 0), (begin, 2 * SPAN - begin))
                    )
        product_grad = product_grad + jnp.pad(
            collected, ((0, 0), (0, 0), (1 + row_step, 1 - row_step), (0, 0))
        )
    weight_f32 = flat_weight.astype(jnp.float32)
    field_grad = jnp.dot(
        weight_f32.T,
        product_grad.reshape(basis_count * variables, -1),
        precision=lax.Precision.HIGHEST,
    )
    field_grad = field_grad.reshape(channels, parallel_number + 2, extended_width)
    full_grad = jnp.pad(
        field_grad, ((0, 0), (0, 0), (offset, refined.shape[-1] - offset - extended_width))
    )
    paired = full_grad.reshape(channels, parallel_number + 2, -1, 2)
    even_part = paired[..., 0]
    odd_part = paired[..., 1]
    sector_grad = jnp.pad(even_part + 0.5 * odd_part, ((0, 0), (0, 0), (0, 1))) + jnp.pad(
        0.5 * odd_part, ((0, 0), (0, 0), (1, 0))
    )
    left_rim = sector_grad[..., :margin]
    right_rim = sector_grad[..., margin + latent_cols :]
    middle = sector_grad[..., margin : margin + latent_cols]
    from_right = lon_send(left_rim, -1)
    from_left = lon_send(right_rim, 1)
    middle = middle + jnp.pad(from_left, ((0, 0), (0, 0), (0, latent_cols - margin)))
    middle = middle + jnp.pad(from_right, ((0, 0), (0, 0), (latent_cols - margin, 0)))
    from_above = lat_send(middle[:, parallel_number + 1], 1)
    from_below = lat_send(middle[:, 0], -1)
    interior = middle[:, 1 : parallel_number + 1]
    interior = interior.at[:, 0].add(from_above)
    interior = interior.at[:, parallel_number - 1].add(from_below)
    return interior[None]


def solution(mesh):
    return jax.shard_map(
        on_device,
        mesh=mesh,
        in_specs=(
            P("ens", None, "lat", "lon"),
            P(),
            P(None, "lat"),
            P(None, "lat", "lon"),
            P(None, "lat", "lon"),
            P("lat"),
        ),
        out_specs=P("ens", None, "lat", "lon"),
        check_vma=False,
    )
```

profile of v0, /device:TPU:64, one launch (start us, length us, event | category | flops | bytes accessed | tf_op | source)
XLA Modules:
  0.0 126.7 jit_solution(7669331909774951162)
XLA Ops:
  0.0 1.3 %fusion.39 = (bf16[90,1,360]{2,1,0:T(2,128)(2,1)S(1)}, bf16[90,1,360]{2,1,0:T(2,128)(2,1)S(1)}) fusion(bf16[90,2,360]{2,1,0:T(2,128)(2,1)} %bitcast.67), kind=kLoop, calls=%fused_computation.131 | loop fusion | bytes 259200 | tf_op jit(solution)/shard_map/slice | solution.py:32
  1.3 4.3 %collective-permute-start = (bf16[90,1,360]{2,1,0:T(2,128)(2,1)S(1)}, bf16[90,1,360]{2,1,0:T(2,128)(2,1)S(1)}, u32[]{:S(2)}, u32[]{:S(2)}) collective-permute-start(bf16[90,1,360]{2,1,0:T(2,128)(2,1)S(1)} %get-tuple-element.57), channel_id=1, source_target_pairs={{0,2},{2,4},{4,6},{6,8},{8,10},{10,12},{12,14},{14,16},{16,18},{18... | collective-permute-start | bytes 194408 | tf_op jit(solution)/shard_map/ppermute | solution.py:31
  5.6 3.9 %collective-permute-start.1 = (bf16[90,1,360]{2,1,0:T(2,128)(2,1)S(1)}, bf16[90,1,360]{2,1,0:T(2,128)(2,1)S(1)}, u32[]{:S(2)}, u32[]{:S(2)}) collective-permute-start(bf16[90,1,360]{2,1,0:T(2,128)(2,1)S(1)} %get-tuple-element.58), channel_id=1, source_target_pairs={{2,0},{4,2},{6,4},{8,6},{10,8},{12,10},{14,12},{16,14},{18,16},{20... | collective-permute-start | bytes 194408 | tf_op jit(solution)/shard_map/ppermute | solution.py:34
  10.6 2.6 %collective-permute-done.1 = bf16[90,1,360]{2,1,0:T(2,128)(2,1)S(1)} collective-permute-done((bf16[90,1,360]{2,1,0:T(2,128)(2,1)S(1)}, bf16[90,1,360]{2,1,0:T(2,128)(2,1)S(1)}, u32[]{:S(2)}, u32[]{:S(2)}) %collective-permute-start.1) | collective-permute-done | bytes 64832 | tf_op jit(solution)/shard_map/ppermute | solution.py:34
  13.7 1.9 %collective-permute-start.2 = (bf16[90,4,3]{2,1,0:T(4,128)(2,1)S(1)}, bf16[90,4,3]{2,1,0:T(4,128)(2,1)S(1)}, u32[]{:S(2)}, u32[]{:S(2)}) collective-permute-start(bf16[90,4,3]{2,1,0:T(4,128)(2,1)S(1)} %get-tuple-element.55), channel_id=1, source_target_pairs={{0,1},{1,0},{2,3},{3,2},{4,5},{5,4},{6,7},{7,6},{8,9},{9,8},{10,11... | collective-permute-start | bytes 6488 | tf_op jit(solution)/shard_map/ppermute | solution.py:31
  15.6 2.4 %collective-permute-start.3 = (bf16[90,4,3]{2,1,0:T(4,128)(2,1)S(1)}, bf16[90,4,3]{2,1,0:T(4,128)(2,1)S(1)}, u32[]{:S(2)}, u32[]{:S(2)}) collective-permute-start(bf16[90,4,3]{2,1,0:T(4,128)(2,1)S(1)} %get-tuple-element.56), channel_id=1, source_target_pairs={{1,0},{0,1},{3,2},{2,3},{5,4},{4,5},{7,6},{6,7},{9,8},{8,9},{11,10... | collective-permute-start | bytes 6488 | tf_op jit(solution)/shard_map/ppermute | solution.py:34
  20.7 1.1 copy.32
  22.1 1.1 copy.33
  25.1 4.2 %fusion.28 = (f32[10,2,720]{2,1,0:T(2,128)S(1)}, f32[10,2,720]{2,1,0:T(2,128)S(1)}) fusion(f32[9,10,4,728]{3,2,1,0:T(4,128)S(1)} %reshape.383, pred[2]{0:T(512)(128)(4,1)S(1)} %get-tuple-element.43, pred[2]{0:T(512)(128)(4,1)S(1)} %get-tuple-element.42, pred[2]{0:T(512)(128)(4,1)S(1)} %get-tuple-element.49, f32[9,2,720]{2,1,0:T(2,128)S(1)} %get-tuple-element.120, ...), kind=kLoop, calls=%fused_computation.76 | loop fusion | flops 1267200 | bytes 4366086 | tf_op jit(solution)/shard_map/reduce_sum | solution.py:120
  29.3 4.8 %fusion.30 = (f32[10,2,720]{2,1,0:T(2,128)S(1)}, f32[10,2,720]{2,1,0:T(2,128)S(1)}, f32[10,2,720]{2,1,0:T(2,128)S(1)}) fusion(f32[9,10,4,728]{3,2,1,0:T(4,128)S(1)} %reshape.383, pred[2]{0:T(512)(128)(4,1)S(1)} %get-tuple-element.46, pred[2]{0:T(512)(128)(4,1)S(1)} %get-tuple-element.45, pred[2]{0:T(512)(128)(4,1)S(1)} %get-tuple-element.48, ...), kind=kLoop, calls=%fused_computation.78 | loop fusion | flops 1512000 | bytes 4993926 | tf_op jit(solution)/shard_map/reduce_sum | solution.py:120
  34.2 5.6 %fusion.26 = (f32[10,2,720]{2,1,0:T(2,128)S(1)}, f32[10,2,720]{2,1,0:T(2,128)S(1)}, f32[10,2,720]{2,1,0:T(2,128)S(1)}, f32[10,2,720]{2,1,0:T(2,128)S(1)}) fusion(f32[9,10,4,728]{3,2,1,0:T(4,128)S(1)} %reshape.383, pred[2]{0:T(512)(128)(4,1)S(1)} %get-tuple-element.41, pred[2]{0:T(512)(128)(4,1)S(1)} %get-tuple-element.40, ...), kind=kLoop, calls=%fused_computation.74 | loop fusion | flops 1756800 | bytes 5621766 | tf_op jit(solution)/shard_map/reduce_sum | solution.py:120
  40.5 38.7 %all_to_all.5 = f32[16,1,10,1440]{3,1,2,0:T(1,128)S(1)} all-to-all(f32[16,1,10,1440]{3,1,2,0:T(1,128)S(1)} %broadcast_in_dim.240), channel_id=1, replica_groups=mesh['ens'=16,'lat'=16,'lon'=2] {'ens'}, dimensions={0} | all-to-all | bytes 1843200 | tf_op jit(solution)/shard_map/all_to_all | solution.py:47
  80.1 1.3 %multiply_select_fusion.3 = (f32[9,10,2,720]{3,2,1,0:T(2,128)S(1)}, f32[9,10,2,720]{3,2,1,0:T(2,128)S(1)}, f32[9,10,2,720]{3,2,1,0:T(2,128)S(1)}, f32[9,10,2,720...) fusion(pred[2]{0:T(512)(128)(4,1)S(1)} %get-tuple-element.47, ...), kind=kLoop, calls=%fused_computation.6 | loop fusion | flops 1296000 | bytes 4308488 | tf_op jit(solution)/shard_map/jit(_where)/select_n | solution.py:151
  81.4 3.2 %multiply_select_fusion.19 = (f32[9,10,2,720]{3,2,1,0:T(2,128)S(1)}, f32[9,10,2,720]{3,2,1,0:T(2,128)S(1)}, f32[9,10,2,720]{3,2,1,0:T(2,128)S(1)}, f32[9,10,2,72...) fusion(pred[2]{0:T(512)(128)(4,1)S(1)} %get-tuple-element.38, ...), kind=kLoop, calls=%fused_computation.22 | loop fusion | flops 2980800 | bytes 10270096 | tf_op jit(solution)/shard_map/jit(_where)/select_n | solution.py:151
  84.7 4.7 %pad_add_fusion.3 = f32[9,10,2,728]{3,2,1,0:T(2,128)S(1)} fusion(f32[9,10,2,720]{3,2,1,0:T(2,128)S(1)} %get-tuple-element.64, f32[9,10,2,720]{3,2,1,0:T(2,128)S(1)} %get-tuple-element.65, f32[9,10,2,720]{3,2,1,0:T(2,128)S(1)} %get-tuple-element.66, f32[9,10,2,720]{3,2,1,0:T(2,128)S(1)} %get-tuple-element.63, f32[9,10,2,720]{3,2,1,0:T(2,128)S(1)} %get-tuple-element.95, ...), kind=kLoop, calls=%fused_computation.73 | loop fusion | flops 1048320 | bytes 5189760 | tf_op jit(solution)/shard_map/add | solution.py:152
  89.4 4.8 %pad_add_fusion.2 = f32[9,10,2,728]{3,2,1,0:T(2,128)S(1)} fusion(f32[9,10,2,720]{3,2,1,0:T(2,128)S(1)} %get-tuple-element.103, f32[9,10,2,720]{3,2,1,0:T(2,128)S(1)} %get-tuple-element.102, f32[9,10,2,720]{3,2,1,0:T(2,128)S(1)} %get-tuple-element.101, f32[9,10,2,720]{3,2,1,0:T(2,128)S(1)} %get-tuple-element.104, f32[9,10,2,720]{3,2,1,0:T(2,128)S(1)} %get-tuple-element.96, ...), kind=kLoop, calls=%fused_computation.72 | loop fusion | flops 1048320 | bytes 5189760 | tf_op jit(solution)/shard_map/add | solution.py:152
  94.2 5.0 %pad_add_fusion.1 = f32[9,10,2,728]{3,2,1,0:T(2,128)S(1)} fusion(f32[9,10,2,720]{3,2,1,0:T(2,128)S(1)} %get-tuple-element.80, f32[9,10,2,720]{3,2,1,0:T(2,128)S(1)} %get-tuple-element.81, f32[9,10,2,720]{3,2,1,0:T(2,128)S(1)} %get-tuple-element.82, f32[9,10,2,720]{3,2,1,0:T(2,128)S(1)} %get-tuple-element.79, f32[9,10,2,720]{3,2,1,0:T(2,128)S(1)} %get-tuple-element.105, ...), kind=kLoop, calls=%fused_computation.71 | loop fusion | flops 1048320 | bytes 5189760 | tf_op jit(solution)/shard_map/add | solution.py:152
  102.5 1.2 copy.35
  104.4 1.9 %collective-permute-start.4 = (f32[90,4,3]{0,1,2:T(4,128)S(1)}, f32[90,4,3]{0,1,2:T(4,128)S(1)}, u32[]{:S(2)}, u32[]{:S(2)}) collective-permute-start(f32[90,4,3]{0,1,2:T(4,128)S(1)} %get-tuple-element.50), channel_id=1, source_target_pairs={{1,0},{0,1},{3,2},{2,3},{5,4},{4,5},{7,6},{6,7},{9,8},{8,9},{11,10... | collective-permute-start | bytes 12968 | tf_op jit(solution)/shard_map/ppermute | solution.py:15
  106.3 2.4 %collective-permute-start.5 = (f32[90,4,3]{0,1,2:T(4,128)S(1)}, f32[90,4,3]{0,1,2:T(4,128)S(1)}, u32[]{:S(2)}, u32[]{:S(2)}) collective-permute-start(f32[90,4,3]{0,1,2:T(4,128)S(1)} %get-tuple-element.51), channel_id=1, source_target_pairs={{1,0},{0,1},{3,2},{2,3},{5,4},{4,5},{7,6},{6,7},{9,8},{8,9},{11,10... | collective-permute-start | bytes 12968 | tf_op jit(solution)/shard_map/ppermute | solution.py:15
  110.3 5.5 %collective-permute-start.6 = (f32[90,360]{0,1:T(8,128)S(1)}, f32[90,360]{0,1:T(8,128)S(1)}, u32[]{:S(2)}, u32[]{:S(2)}) collective-permute-start(f32[90,360]{0,1:T(8,128)S(1)} %bitcast.72), channel_id=1, source_target_pairs={{0,2},{2,4},{4,6},{6,8},{8,10},{10,12},{12,14},{14,16},{16,18},{18... | collective-permute-start | bytes 388808 | tf_op jit(solution)/shard_map/ppermute | solution.py:21
  116.0 1.9 %collective-permute-start.7 = (f32[90,360]{0,1:T(8,128)S(1)}, f32[90,360]{0,1:T(8,128)S(1)}, u32[]{:S(2)}, u32[]{:S(2)}) collective-permute-start(f32[90,360]{0,1:T(8,128)S(1)} %bitcast.71), channel_id=1, source_target_pairs={{2,0},{4,2},{6,4},{8,6},{10,8},{12,10},{14,12},{16,14},{18,16},{20... | collective-permute-start | bytes 388808 | tf_op jit(solution)/shard_map/ppermute | solution.py:21
  118.0 2.2 %collective-permute-done.6 = f32[90,360]{0,1:T(8,128)S(1)} collective-permute-done((f32[90,360]{0,1:T(8,128)S(1)}, f32[90,360]{0,1:T(8,128)S(1)}, u32[]{:S(2)}, u32[]{:S(2)}) %collective-permute-start.6) | collective-permute-done | bytes 129632 | tf_op jit(solution)/shard_map/ppermute | solution.py:21
  120.2 5.5 %collective-permute-done.7 = f32[90,360]{0,1:T(8,128)S(1)} collective-permute-done((f32[90,360]{0,1:T(8,128)S(1)}, f32[90,360]{0,1:T(8,128)S(1)}, u32[]{:S(2)}, u32[]{:S(2)}) %collective-permute-start.7) | collective-permute-done | bytes 129632 | tf_op jit(solution)/shard_map/ppermute | solution.py:21
  (55 shorter events, 14.6 us)
Async XLA Ops:
  0.0 13.2 %copy-start = (bf16[1,90,2,360]{3,2,1,0:T(2,128)(2,1)S(1)}, bf16[1,90,2,360]{3,2,1,0:T(2,128)(2,1)}, u32[]{:S(2)}) copy-start(bf16[1,90,2,360]{3,2,1,0:T(2,128)(2,1)} %param.10) | copy-start | bytes 388804
  0.0 18.0 %copy-start.3 = (s32[3,2]{0,1:T(2,128)S(1)}, s32[3,2]{0,1:T(2,128)}, u32[]{:S(2)}) copy-start(s32[3,2]{0,1:T(2,128)} %param.12) | copy-start | bytes 76
  0.0 18.4 %copy-start.2 = (bf16[9,10,90]{2,1,0:T(8,128)(2,1)S(1)}, bf16[9,10,90]{2,1,0:T(8,128)(2,1)}, u32[]{:S(2)}) copy-start(bf16[9,10,90]{2,1,0:T(8,128)(2,1)} %param.11) | copy-start | bytes 48604
  1.3 9.3 %collective-permute-start = (bf16[90,1,360]{2,1,0:T(2,128)(2,1)S(1)}, bf16[90,1,360]{2,1,0:T(2,128)(2,1)S(1)}, u32[]{:S(2)}, u32[]{:S(2)}) collective-permute-start(bf16[90,1,360]{2,1,0:T(2,128)(2,1)S(1)} %get-tuple-element.57), channel_id=1, source_target_pairs={{0,2},{2,4},{4,6},{6,8},{8,10},{10,12},{12,14},{14,16},{16,18},{18... | collective-permute-start | bytes 194408 | tf_op jit(solution)/shard_map/ppermute | solution.py:31
  5.6 7.6 %collective-permute-start.1 = (bf16[90,1,360]{2,1,0:T(2,128)(2,1)S(1)}, bf16[90,1,360]{2,1,0:T(2,128)(2,1)S(1)}, u32[]{:S(2)}, u32[]{:S(2)}) collective-permute-start(bf16[90,1,360]{2,1,0:T(2,128)(2,1)S(1)} %get-tuple-element.58), channel_id=1, source_target_pairs={{2,0},{4,2},{6,4},{8,6},{10,8},{12,10},{14,12},{16,14},{18,16},{20... | collective-permute-start | bytes 194408 | tf_op jit(solution)/shard_map/ppermute | solution.py:34
  13.7 4.7 %collective-permute-start.2 = (bf16[90,4,3]{2,1,0:T(4,128)(2,1)S(1)}, bf16[90,4,3]{2,1,0:T(4,128)(2,1)S(1)}, u32[]{:S(2)}, u32[]{:S(2)}) collective-permute-start(bf16[90,4,3]{2,1,0:T(4,128)(2,1)S(1)} %get-tuple-element.55), channel_id=1, source_target_pairs={{0,1},{1,0},{2,3},{3,2},{4,5},{5,4},{6,7},{7,6},{8,9},{9,8},{10,11... | collective-permute-start | bytes 6488 | tf_op jit(solution)/shard_map/ppermute | solution.py:31
  15.6 3.3 %collective-permute-start.3 = (bf16[90,4,3]{2,1,0:T(4,128)(2,1)S(1)}, bf16[90,4,3]{2,1,0:T(4,128)(2,1)S(1)}, u32[]{:S(2)}, u32[]{:S(2)}) collective-permute-start(bf16[90,4,3]{2,1,0:T(4,128)(2,1)S(1)} %get-tuple-element.56), channel_id=1, source_target_pairs={{1,0},{0,1},{3,2},{2,3},{5,4},{4,5},{7,6},{6,7},{9,8},{8,9},{11,10... | collective-permute-start | bytes 6488 | tf_op jit(solution)/shard_map/ppermute | solution.py:34
  79.2 0.8 copy-start.1
  79.2 0.8 copy-start.4
  104.4 4.3 %collective-permute-start.4 = (f32[90,4,3]{0,1,2:T(4,128)S(1)}, f32[90,4,3]{0,1,2:T(4,128)S(1)}, u32[]{:S(2)}, u32[]{:S(2)}) collective-permute-start(f32[90,4,3]{0,1,2:T(4,128)S(1)} %get-tuple-element.50), channel_id=1, source_target_pairs={{1,0},{0,1},{3,2},{2,3},{5,4},{4,5},{7,6},{6,7},{9,8},{8,9},{11,10... | collective-permute-start | bytes 12968 | tf_op jit(solution)/shard_map/ppermute | solution.py:15
  106.3 3.2 %collective-permute-start.5 = (f32[90,4,3]{0,1,2:T(4,128)S(1)}, f32[90,4,3]{0,1,2:T(4,128)S(1)}, u32[]{:S(2)}, u32[]{:S(2)}) collective-permute-start(f32[90,4,3]{0,1,2:T(4,128)S(1)} %get-tuple-element.51), channel_id=1, source_target_pairs={{1,0},{0,1},{3,2},{2,3},{5,4},{4,5},{7,6},{6,7},{9,8},{8,9},{11,10... | collective-permute-start | bytes 12968 | tf_op jit(solution)/shard_map/ppermute | solution.py:15
  110.3 9.9 %collective-permute-start.6 = (f32[90,360]{0,1:T(8,128)S(1)}, f32[90,360]{0,1:T(8,128)S(1)}, u32[]{:S(2)}, u32[]{:S(2)}) collective-permute-start(f32[90,360]{0,1:T(8,128)S(1)} %bitcast.72), channel_id=1, source_target_pairs={{0,2},{2,4},{4,6},{6,8},{8,10},{10,12},{12,14},{14,16},{16,18},{18... | collective-permute-start | bytes 388808 | tf_op jit(solution)/shard_map/ppermute | solution.py:21
  116.0 9.7 %collective-permute-start.7 = (f32[90,360]{0,1:T(8,128)S(1)}, f32[90,360]{0,1:T(8,128)S(1)}, u32[]{:S(2)}, u32[]{:S(2)}) collective-permute-start(f32[90,360]{0,1:T(8,128)S(1)} %bitcast.71), channel_id=1, source_target_pairs={{2,0},{4,2},{6,4},{8,6},{10,8},{12,10},{14,12},{16,14},{18,16},{20... | collective-permute-start | bytes 388808 | tf_op jit(solution)/shard_map/ppermute | solution.py:21
where the time goes:
time: 127 us
  blocking collectives  38.7 us (30%)
  other arithmetic  38.6 us (30%)
  starting transfers between devices  24.3 us (19%)
  local copies, waits for them, and re-layouts  12 us (9%)
  waiting for transfers between devices  11.7 us (9%)
    all_to_all x1, blocking collectives, from_everyone(): lax.all_to_all(jnp.broadcast_to(array[None], (count, *array.shape)), axis...  38.7 us
    reduce_sum x3, other arithmetic, on_device(): prediction = prediction + jnp.sum(picked_function[:, None] * picked, axis=0)  14.7 us
    add x3, other arithmetic, on_device(): collected + jnp.pad(masked, ((0, 0), (0, 0), (0, 0), (begin, 2 * SPAN - b...  14.6 us
    ppermute x2, waiting for transfers between devices, shifted(): return lax.ppermute(array, axis, pairs)  7.73 us
    ppermute x2, starting transfers between devices, shifted(): return lax.ppermute(array, axis, pairs)  7.41 us
    ppermute x2, starting transfers between devices, padded(): lax.ppermute(lax.slice_in_dim(block, 0, width, axis=dim), axis, backward)  6.33 us
    ppermute x2, starting transfers between devices, padded(): lax.ppermute(lax.slice_in_dim(block, block.shape[dim] - width, None, axis...  6.2 us
    select_n x2, other arithmetic, on_device(): masked = jnp.where(row_stride == stride_value, sample_dispersion, 0.0)  4.51 us
  transfers between devices with their start and end apart: 8, of which 5 were waited for; matrix products, arithmetic and copies ran while one was open for 1% of the time, Pallas kernels for 0%

commit v1 on v0

v1 whole, which is shorter than its diff:
```python
import functools

import jax
import jax.numpy as jnp
import numpy as np
from jax import lax
from jax.experimental import pallas as pl
from jax.experimental.pallas import tpu as pltpu
from jax.sharding import PartitionSpec as P

SPAN = 4
BASES = 9
LANES = 384
TILE = 128
ROWS = 24
SMOOTH = 0.01
F32 = jnp.float32
BF16 = jnp.bfloat16
MESH = pl.DeviceIdType.MESH


def expand_picks():
    rows = np.zeros((112, 32), np.float32)
    for slot in range(9):
        a = slot // 3 - 1
        for sub in range(8):
            q = (sub & 1) - a
            if 0 <= q <= 1:
                rows[8 * slot + sub, 2 * slot + q] = 1
    for i in range(3):
        rows[72 + i, 2 * i] = 1
        rows[80 + i, 2 * (6 + i) + 1] = 1
        rows[88 + 3 + i, 2 * i] = 1
        rows[96 + 3 + i, 2 * (6 + i) + 1] = 1
    return rows


def expand_weights():
    rows = np.zeros((BASES * ROWS, 96), np.float32)
    for k in range(BASES):
        for v in range(10):
            for p in range(2):
                rows[ROWS * k + 2 * v + p, 10 * k + v] = 1
    return rows


def iota(shape, dim):
    return lax.broadcasted_iota(jnp.int32, shape, dim)


def lane_roll(x, by):
    by %= x.shape[-1]
    return x if by == 0 else pltpu.roll(x, by, axis=x.ndim - 1)


def row_down(x):
    return pltpu.roll(x, 1, axis=x.ndim - 2)


def row_up(x):
    return pltpu.roll(x, x.shape[-2] - 1, axis=x.ndim - 2)


def smoothed_derivative(d):
    return d * lax.rsqrt(d * d + SMOOTH)


def shifted(pair, sign, steps):
    rolled = {}

    def at(parity, by):
        if (parity, by) not in rolled:
            rolled[parity, by] = lane_roll(pair[parity], -by)
        return rolled[parity, by]

    steps = jnp.broadcast_to(steps, pair[0].shape)
    out = []
    for parity in (0, 1):
        result = None
        for n in range(1, SPAN + 1):
            column = parity + sign * n
            value = at(column % 2, column // 2)
            result = value if result is None else jnp.where(steps == float(n), value, result)
        out.append(result)
    return out


def edge_of(x):
    lane = iota((*x.shape[:-1], TILE), x.ndim - 1)
    return jnp.where(lane < 64, x[..., :TILE], x[..., 2 * TILE :])


def extended(x, edge):
    lane = iota(edge.shape, edge.ndim - 1)
    last = jnp.where(
        lane < 104, x[..., 2 * TILE :], jnp.where(lane < 112, lane_roll(edge, 104), lane_roll(edge, 24))
    )
    return jnp.concatenate([x[..., : 2 * TILE], last], axis=-1)


def kernel(
    nx, ny, nlat, off_ref, cos_ref, x_ref, w_ref, pk_ref, obs_ref, s1_ref, ex_ref, out_ref,
    xpar, prod, qp, mask, csum, fsel, pgrad, su, sd, ru, rd, zu, zd, rzu, rzd,
    qpe, rqpe, own, yblk, xblk, fe, rfe, f0, f1, r0, r1, f0e, f1e, r0e, r1e, send_sem, recv_sem,
):
    ens = lax.axis_index("ens")
    lat = lax.axis_index("lat")
    lon = lax.axis_index("lon")
    ex, ey = ens // ny, ens % ny
    up = (lat + nlat - 1) % nlat
    down = (lat + 1) % nlat
    partner = 1 - lon
    have_up = jnp.where(lat > 0, 1.0, 0.0).astype(F32)
    have_down = jnp.where(lat < nlat - 1, 1.0, 0.0).astype(F32)

    def x_peer(d):
        return ((ex + d) % nx) * ny + ey

    def y_peer(d):
        return ex * ny + (ey + d) % ny

    def target(e=None, t=None, n=None):
        return (ens if e is None else e, lat if t is None else t, lon if n is None else n)

    sems = [0]

    def remote(src, dst, device):
        i = sems[0]
        sems[0] += 1
        return pltpu.make_async_remote_copy(
            src_ref=src, dst_ref=dst, send_sem=send_sem.at[i], recv_sem=recv_sem.at[i],
            device_id=device, device_id_type=MESH,
        )

    barrier = pltpu.get_barrier_semaphore()
    peers = [target(n=partner)]
    peers += [target(t=t, n=n) for t in (up, down) for n in (lon, partner)]
    peers += [target(e=x_peer(d)) for d in range(1, nx)] + [target(e=y_peer(d)) for d in range(1, ny)]
    for device in peers:
        pl.semaphore_signal(barrier, inc=1, device_id=device, device_id_type=MESH)

    pick = iota((256, 256), 0) - 2 * iota((256, 256), 1)
    half = iota((256, 256), 1)
    select = jnp.where((pick == jnp.where(half < TILE, 0, -255)), 1.0, 0.0).astype(BF16)
    rows = jnp.dot(ex_ref[...], pk_ref[...], preferred_element_type=F32).astype(BF16)
    obs = obs_ref[...]
    obs_hi = obs.astype(BF16)
    obs_lo = (obs - obs_hi.astype(F32)).astype(BF16)
    obs_e, obs_o = [], []
    row8 = iota((8, TILE), 0)
    for block in range(3):
        wide = slice(256 * block, 256 * block + 256)
        tile = slice(TILE * block, TILE * block + TILE)
        got = jnp.dot(rows[:, wide], select, preferred_element_type=F32)
        for slot in range(9):
            qp[0, slot, :, tile] = got[8 * slot : 8 * slot + 8, :TILE]
            qp[1, slot, :, tile] = got[8 * slot : 8 * slot + 8, TILE:]
        su[:, tile] = jnp.where(row8 == 6, off_ref[0, 0], got[72:80, :TILE] + got[88:96, TILE:])
        sd[:, tile] = jnp.where(row8 == 6, off_ref[2, 1], got[80:88, :TILE] + got[96:104, TILE:])
        both = jnp.dot(obs_hi[:, wide], select, preferred_element_type=F32) + jnp.dot(
            obs_lo[:, wide], select, preferred_element_type=F32
        )
        obs_e.append(both[:, :TILE])
        obs_o.append(both[:, TILE:])
    obs = jnp.concatenate([jnp.concatenate(obs_e, axis=1), jnp.concatenate(obs_o, axis=1)], axis=0)

    pl.semaphore_wait(barrier, len(peers))
    started = []

    def go(src, dst, device):
        copy = remote(src, dst, device)
        copy.start()
        started.append(copy)
        return copy

    c_x = go(x_ref, xpar, target(n=partner))
    c_up = go(su, rd, target(t=up))
    c_down = go(sd, ru, target(t=down))

    spread = jnp.dot(s1_ref[...], w_ref[...], preferred_element_type=F32).astype(BF16)
    s2 = jnp.where(iota((TILE, 192), 1) // 2 == iota((TILE, 192), 0), 1.0, 0.0).astype(BF16)
    wf = jnp.dot(spread, s2, preferred_element_type=F32)
    wf = jnp.where(iota(wf.shape, 0) % 2 == iota(wf.shape, 1) % 2, wf, 0.0).astype(BF16)
    s2t = jnp.where(iota((192, TILE), 0) // 2 == iota((192, TILE), 1), 1.0, 0.0).astype(BF16)
    wb = lax.dot_general(s2t, spread, (((1,), (1,)), ((), ())), preferred_element_type=F32)
    wb = jnp.where(iota(wb.shape, 0) % 2 == iota(wb.shape, 1) % 2, wb, 0.0).astype(BF16)

    c_x.wait_recv()
    latent = extended(x_ref[...].astype(F32), edge_of(xpar[...].astype(F32)))
    halfway = 0.5 * (latent + lane_roll(latent, -1))
    for parity, x in enumerate((latent, halfway)):
        got = jnp.dot(wf, x.astype(BF16), preferred_element_type=F32)
        prod[parity] = got.reshape(BASES, 3, 8, LANES)

    c_up.wait_recv()
    c_down.wait_recv()
    even = iota((8, LANES), 0) % 2 == 0

    def spread_row(ref, i):
        return jnp.broadcast_to(ref[i : i + 1, :], (8, LANES))

    steps = {
        -1: jnp.where(even, off_ref[0, 1], spread_row(rd, 6)),
        0: None,
        1: jnp.where(even, spread_row(ru, 6), off_ref[2, 0]),
    }
    own0 = jnp.where(even, off_ref[1, 0], off_ref[1, 1])
    steps[0] = own0
    for parity in (0, 1):
        for i in range(3):
            qp[parity, 6 + i] = jnp.where(even, spread_row(ru, 3 * parity + i), qp[parity, 6 + i])
            qp[parity, i] = jnp.where(even, qp[parity, i], spread_row(rd, 3 * parity + i))
    for parity in (0, 1):
        qpe[parity] = edge_of(qp[parity])
    c_q = go(qpe, rqpe, target(n=partner))

    def build_masks(source):
        for a in (-1, 0, 1):
            for b in (-1, 0, 1):
                slot = 3 * (a + 1) + b + 1
                pair = source(slot)
                if b:
                    pair = shifted(pair, -b, steps[a])
                for parity in (0, 1):
                    mask[parity, slot] = pair[parity]

    build_masks(lambda slot: [qp[0, slot], qp[1, slot]])

    for parity in (0, 1):
        for t in range(3):
            tile = slice(TILE * t, TILE * t + TILE)
            values = [prod[parity, k, :, :, tile] for k in range(BASES)]
            for slot in range(9):
                want = jnp.broadcast_to(mask[parity, slot, :, tile][None], (3, 8, TILE))
                total = jnp.where(want == 0.0, values[0], 0.0)
                for k in range(1, BASES):
                    total = jnp.where(want == float(k), values[k], total)
                csum[parity, slot, :, :, tile] = total

    def target_sum(a):
        total = [csum[0, 3 * (a + 1) + 1], csum[1, 3 * (a + 1) + 1]]
        for b in (-1, 1):
            slot = 3 * (a + 1) + b + 1
            moved = shifted([csum[0, slot], csum[1, slot]], b, steps[a])
            total = [x + y for x, y in zip(total, moved)]
        return total

    even3 = iota((3, 8, LANES), 1) % 2 == 0
    to_up = target_sum(1)
    to_down = target_sum(-1)
    zu[...] = jnp.where(even3, to_up[0], row_down(to_up[1]))
    zd[...] = jnp.where(even3, row_up(to_down[0]), to_down[1])
    c_zu = go(zu, rzu, target(t=up))
    c_zd = go(zd, rzd, target(t=down))
    middle = target_sum(0)
    local = [
        middle[parity] + jnp.where(even3, row_up(to_up[parity]), row_down(to_down[parity])) for parity in (0, 1)
    ]
    c_zu.wait_recv()
    c_zd.wait_recv()
    from_down = rzu[...] * have_down
    from_up = rzd[...] * have_up
    pred = [
        local[0] + jnp.where(even3, from_up, row_down(from_down)),
        local[1] + jnp.where(even3, row_up(from_up), from_down),
    ]
    pred = jnp.concatenate([x.reshape(ROWS, LANES) for x in pred], axis=0)
    own[...] = pred.astype(BF16)

    c_y = [go(own, yblk.at[d - 1], target(e=y_peer(d))) for d in range(1, ny)]
    c_xs = [go(own, xblk.at[0, d - 1], target(e=x_peer(d))) for d in range(1, nx)]
    pair_total = jnp.zeros_like(pred)
    relayed = [c_xs]
    for d in range(1, ny):
        c_y[d - 1].wait_recv()
        relayed.append([go(yblk.at[d - 1], xblk.at[d, e - 1], target(e=x_peer(e))) for e in range(1, nx)])

    c_q.wait_recv()
    build_masks(lambda slot: [extended(qp[parity, slot], rqpe[parity, slot]) for parity in (0, 1)])

    for d in range(1, ny):
        pair_total += smoothed_derivative(pred - yblk[d - 1].astype(F32))
    for d in range(ny):
        for e in range(1, nx):
            relayed[d][e - 1].wait_recv()
            pair_total += smoothed_derivative(pred - xblk[d, e - 1].astype(F32))

    factor = jnp.where(iota(pred.shape, 0) % 2 == 0, cos_ref[0], cos_ref[1])
    grad = factor * (smoothed_derivative(pred - obs) - pair_total * (1.0 / (nx * ny - 1)))
    grad = [grad[:ROWS].reshape(3, 8, LANES), grad[ROWS:].reshape(3, 8, LANES)]
    f0[...] = jnp.where(even3, grad[0], row_down(grad[1]))
    f1[...] = jnp.where(even3, row_up(grad[0]), grad[1])
    f0e[...] = edge_of(f0[...])
    f1e[...] = edge_of(f1[...])
    for parity in (0, 1):
        fe[parity] = edge_of(grad[parity])
    c_f = [
        go(f0, r0, target(t=up)),
        go(f1, r1, target(t=down)),
        go(f0e, r0e, target(t=up, n=partner)),
        go(f1e, r1e, target(t=down, n=partner)),
        go(fe, rfe, target(n=partner)),
    ]

    def around(own_pair, below, above):
        is_even = iota(below.shape, 1) % 2 == 0
        return {
            1: [
                jnp.where(is_even, above, row_down(own_pair[0])),
                jnp.where(is_even, row_up(above), row_down(own_pair[1])),
            ],
            0: own_pair,
            -1: [
                jnp.where(is_even, row_up(own_pair[0]), row_down(below)),
                jnp.where(is_even, row_up(own_pair[1]), below),
            ],
        }

    for copy in c_f:
        copy.wait_recv()
    seen = around(grad, r0[...] * have_down, r1[...] * have_up)
    edges = around([rfe[0], rfe[1]], r0e[...] * have_down, r1e[...] * have_up)
    for a in (-1, 0, 1):
        wide = [extended(x, edge) for x, edge in zip(seen[a], edges[a])]
        for b in (-1, 0, 1):
            slot = 3 * (a + 1) + b + 1
            pair = shifted(wide, -b, steps[a]) if b else wide
            for parity in (0, 1):
                fsel[parity, slot] = pair[parity]

    for parity in (0, 1):
        for t in range(3):
            tile = slice(TILE * t, TILE * t + TILE)
            values = [fsel[parity, slot, :, :, tile] for slot in range(9)]
            wants = [jnp.broadcast_to(mask[parity, slot, :, tile][None], (3, 8, TILE)) for slot in range(9)]
            for k in range(BASES):
                total = jnp.where(wants[0] == float(k), values[0], 0.0)
                for slot in range(1, 9):
                    total = total + jnp.where(wants[slot] == float(k), values[slot], 0.0)
                pgrad[parity, k, :, :, tile] = total

    odd = pgrad[1].reshape(BASES * ROWS, LANES)
    folded = pgrad[0].reshape(BASES * ROWS, LANES) + 0.5 * (odd + lane_roll(odd, 1))
    out_ref[...] = jnp.dot(wb, folded.astype(BF16), preferred_element_type=F32)

    for copy in started:
        copy.wait_send()


def on_device(sizes, hidden_state, filter_coefficients, meridian_offset_table, function_pick_table, observation, latitude_cosine_factor):
    nx, ny, nlat = sizes
    channels = hidden_state.shape[1]
    columns = hidden_state.shape[3]
    x = jnp.pad(hidden_state.reshape(2 * channels, columns), ((0, 192 - 2 * channels), (0, LANES - columns)))
    weights = jnp.pad(filter_coefficients.reshape(90, 90), ((0, 6), (0, 38)))
    picks = jnp.pad(function_pick_table.reshape(18, 2 * columns).astype(BF16), ((0, 14), (0, 768 - 2 * columns)))
    obs = jnp.pad(observation.reshape(20, 2 * columns), ((0, 4), (0, 768 - 2 * columns)))
    smem = pl.BlockSpec(memory_space=pltpu.SMEM)
    vmem = pl.BlockSpec(memory_space=pltpu.VMEM)
    row = pltpu.VMEM((8, LANES), F32)
    field = pltpu.VMEM((3, 8, LANES), F32)
    edge = pltpu.VMEM((3, 8, TILE), F32)
    copies = 11 + (ny - 1) + ny * (nx - 1)
    out = pl.pallas_call(
        functools.partial(kernel, nx, ny, nlat),
        out_shape=jax.ShapeDtypeStruct((192, LANES), F32),
        in_specs=[smem, smem] + [vmem] * 6,
        out_specs=vmem,
        scratch_shapes=[
            pltpu.VMEM((192, LANES), BF16),
            pltpu.VMEM((2, 9, 3, 8, LANES), F32),
            pltpu.VMEM((2, 9, 8, LANES), F32),
            pltpu.VMEM((2, 9, 8, LANES), F32),
            pltpu.VMEM((2, 9, 3, 8, LANES), F32),
            pltpu.VMEM((2, 9, 3, 8, LANES), F32),
            pltpu.VMEM((2, 9, 3, 8, LANES), F32),
            row, row, row, row,
            field, field, field, field,
            pltpu.VMEM((2, 9, 8, TILE), F32),
            pltpu.VMEM((2, 9, 8, TILE), F32),
            pltpu.VMEM((2 * ROWS, LANES), BF16),
            pltpu.VMEM((ny - 1, 2 * ROWS, LANES), BF16),
            pltpu.VMEM((ny, nx - 1, 2 * ROWS, LANES), BF16),
            pltpu.VMEM((2, 3, 8, TILE), F32),
            pltpu.VMEM((2, 3, 8, TILE), F32),
            field, field, field, field,
            edge, edge, edge, edge,
            pltpu.SemaphoreType.DMA((copies,)),
            pltpu.SemaphoreType.DMA((copies,)),
        ],
        compiler_params=pltpu.CompilerParams(collective_id=0, has_side_effects=True),
    )(
        meridian_offset_table.astype(F32),
        latitude_cosine_factor,
        x,
        weights,
        picks,
        obs,
        jnp.asarray(expand_weights(), BF16),
        jnp.asarray(expand_picks(), BF16),
    )
    return out[: 2 * channels, :columns].reshape(1, channels, 2, columns)


def solution(mesh):
    members = mesh.shape["ens"]
    nx = 4 if members % 4 == 0 and members > 4 else 2
    return jax.shard_map(
        functools.partial(on_device, (nx, members // nx, mesh.shape["lat"])),
        mesh=mesh,
        in_specs=(
            P("ens", None, "lat", "lon"),
            P(),
            P(None, "lat"),
            P(None, "lat", "lon"),
            P(None, "lat", "lon"),
            P("lat"),
        ),
        out_specs=P("ens", None, "lat", "lon"),
        check_vma=False,
    )
```

time: 127 us -> 48.2 us (0.38)
  the two profiles are of different devices: /device:TPU:64 before, /device:TPU:1 now
where the time goes in v1:
time: 48.2 us; the launch traced here: 47.9 us
  Pallas kernels  40.6 us (84%)
  local copies, waits for them, and re-layouts  6.63 us (14%)
  other arithmetic  0.6 us (1%)
    pallas_call x1, Pallas kernels, on_device(): pl.pallas_call(functools.partial(kernel, nx, ny, nlat), out_shape=jax.Sha...  40.6 us
    unnamed x7, local copies, waits for them, and re-layouts  1.15 us
    slice x1, local copies, waits for them, and re-layouts, on_device(): return out[:2 * channels, :columns].reshape(1, channels, 2, columns)  0.98 us

profile of v1, /device:TPU:1, one launch (start us, length us, event | category | flops | bytes accessed | tf_op | source)
XLA Modules:
  0.0 47.9 jit_solution(4424517344828345866)
XLA Ops:
  0.0 0.8 %copy.9 = s32[3,2]{1,0:T(4,128)S(1)} copy(s32[3,2]{0,1:T(2,128)} %param.10) | data formatting | bytes 48 | tf_op args[2]
  0.8 0.6 %convert_element_type.17.off_ref = f32[3,2]{1,0:T(4,128)} convert(s32[3,2]{1,0:T(4,128)S(1)} %copy.9) | non-fusion elementwise | flops 6 | bytes 48 | tf_op jit(solution)/shard_map/convert_element_type | solution.py:393
  1.3 0.0 copy-start.2
  1.3 0.8 %reshape.15 = bf16[90,90]{1,0:T(8,128)(2,1)S(1)} reshape(bf16[9,10,90]{2,1,0:T(8,128)(2,1)} %param.9) | data formatting | bytes 32400 | tf_op jit(solution)/shard_map/reshape | solution.py:355
  2.1 0.6 %pad.17.w_ref = bf16[96,128]{1,0:T(8,128)(2,1)} pad(bf16[90,90]{1,0:T(8,128)(2,1)S(1)} %reshape.15, bf16[]{:T(256)} %constant.7.clone.1), padding=0_6x0_38 | pad | bytes 40778 | tf_op jit(solution)/shard_map/jit(_pad)/pad | solution.py:355
  2.8 0.0 copy-done.2
  2.8 0.0 copy-start.1
  2.9 0.6 %pad.18.pk_ref = bf16[32,768]{1,0:T(8,128)(2,1)} pad(bf16[18,720]{1,0:T(8,128)(2,1)S(1)} %convert_element_type.19, bf16[]{:T(256)} %constant.7.clone.1), padding=0_14x0_48 | pad | bytes 75074 | tf_op jit(solution)/shard_map/jit(_pad)/pad | solution.py:356
  3.5 0.1 copy-done.1
  3.6 0.0 copy-start
  3.7 0.6 %pad.19.obs_ref = f32[24,768]{1,0:T(8,128)} pad(f32[20,720]{1,0:T(8,128)S(1)} %reshape.16, f32[]{:T(128)} %constant.8.clone.1), padding=0_4x0_48 | pad | bytes 131332 | tf_op jit(solution)/shard_map/jit(_pad)/pad | solution.py:357
  4.3 0.2 copy-done
  4.5 0.2 reshape.14
  4.7 0.7 %pad.16.x_ref = bf16[192,384]{1,0:T(8,128)(2,1)} pad(bf16[180,360]{1,0:T(8,128)(2,1)S(1)} %reshape.14, bf16[]{:T(256)} %constant.7.clone.1), padding=0_12x0_24 | pad | bytes 277058 | tf_op jit(solution)/shard_map/jit(_pad)/pad | solution.py:354
  5.4 40.6 %shard_map.82 = f32[192,384]{1,0:T(8,128)} custom-call(f32[3,2]{1,0:T(4,128)} %convert_element_type.17.off_ref, f32[2]{0:T(128)} %cos_ref.1, bf16[192,384]{1,0:T(8,128)(2,1)} %pad.16.x_ref, bf16[96,128]{1,0:T(8,128)(2,1)} %pad.17.w_ref, bf16[32,768]{1,0:T(8,128)(2,1)} %pad.18.pk_ref, f32[24,768]{1,0:T(8,128)} %pad.19.obs_ref, ...), custom_call_target="tpu_custom_call" | custom-call | tf_op jit(solution)/shard_map/pallas_call | solution.py:364
  46.0 1.0 %slice.3 = f32[180,360]{1,0:T(8,128)S(1)} slice(f32[192,384]{1,0:T(8,128)} %shard_map.82), slice={[0:180], [0:360]} | slice | bytes 518400 | tf_op jit(solution)/shard_map/slice | solution.py:402
  47.0 0.9 %reshape.17 = f32[1,90,2,360]{3,2,1,0:T(2,128)} reshape(f32[180,360]{1,0:T(8,128)S(1)} %slice.3) | data formatting | bytes 518400 | tf_op jit(solution)/shard_map/reshape | solution.py:402
  (3 shorter events, 0.1 us)
Async XLA Ops:
  1.3 1.4 %copy-start.2 = (s32[9,2,720]{2,1,0:T(2,128)S(1)}, s32[9,2,720]{2,1,0:T(2,128)}, u32[]{:S(2)}) copy-start(s32[9,2,720]{2,1,0:T(2,128)} %param.11) | copy-start | bytes 155524
  2.8 0.8 %copy-start.1 = (f32[10,2,720]{2,1,0:T(2,128)S(1)}, f32[10,2,720]{2,1,0:T(2,128)}, u32[]{:S(2)}) copy-start(f32[10,2,720]{2,1,0:T(2,128)} %param.12) | copy-start | bytes 172804
  3.6 0.9 %copy-start = (bf16[1,90,2,360]{3,2,1,0:T(2,128)(2,1)S(1)}, bf16[1,90,2,360]{3,2,1,0:T(2,128)(2,1)}, u32[]{:S(2)}) copy-start(bf16[1,90,2,360]{3,2,1,0:T(2,128)(2,1)} %param.8) | copy-start | bytes 388804

commit v2 on v1

v2 whole, which is shorter than its diff:
```python
import functools

import jax
import jax.numpy as jnp
import numpy as np
from jax import lax
from jax.experimental import pallas as pl
from jax.experimental.pallas import tpu as pltpu
from jax.sharding import PartitionSpec as P

SPAN = 4
BASES = 9
LANES = 384
TILE = 128
ROWS = 24
SMOOTH = 0.01
F32 = jnp.float32
BF16 = jnp.bfloat16
MESH = pl.DeviceIdType.MESH
HALO = BF16
SUMS = F32
Y_RELAY = False
X_RELAY = ()


def expand_picks():
    rows = np.zeros((80, 18), np.float32)
    for i in range(3):
        for sub in range(8):
            rows[8 * i + sub, 2 * (3 + i) + (sub & 1)] = 1
            rows[24 + 8 * i + sub, 2 * (6 + i) if sub & 1 else 2 * i + 1] = 1
        rows[48 + i, 2 * i] = 1
        rows[56 + i, 2 * (6 + i) + 1] = 1
        rows[64 + 3 + i, 2 * i] = 1
        rows[72 + 3 + i, 2 * (6 + i) + 1] = 1
    return rows


def iota(shape, dim):
    return lax.broadcasted_iota(jnp.int32, shape, dim)


def swapped(x):
    return jnp.where(iota(x.shape, x.ndim - 2) % 2 == 0, row_up(x), row_down(x))


def packed(pair):
    middle = jnp.where(iota((8, LANES), 0) < 4, pair[0][2], pltpu.roll(pair[1][2], 4, axis=0))
    return jnp.concatenate([pair[0][:2], middle[None], pair[1][:2]], axis=0)


def unpacked(x):
    return [x[:3], jnp.concatenate([x[3:], pltpu.roll(x[2], 4, axis=0)[None]], axis=0)]


def lane_roll(x, by):
    by %= x.shape[-1]
    return x if by == 0 else pltpu.roll(x, by, axis=x.ndim - 1)


def row_down(x):
    return pltpu.roll(x, 1, axis=x.ndim - 2)


def row_up(x):
    return pltpu.roll(x, x.shape[-2] - 1, axis=x.ndim - 2)


def smoothed_derivative(d):
    return d * lax.rsqrt(d * d + SMOOTH)


def shifted(pair, sign, steps):
    rolled = {}

    def at(parity, by):
        if (parity, by) not in rolled:
            rolled[parity, by] = lane_roll(pair[parity], -by)
        return rolled[parity, by]

    steps = jnp.broadcast_to(steps, pair[0].shape)
    out = []
    for parity in (0, 1):
        result = None
        for n in range(1, SPAN + 1):
            column = parity + sign * n
            value = at(column % 2, column // 2)
            result = value if result is None else jnp.where(steps == float(n), value, result)
        out.append(result)
    return out


def edge_of(x):
    lane = iota((*x.shape[:-1], TILE), x.ndim - 1)
    return jnp.where(lane < 64, x[..., :TILE], x[..., 2 * TILE :])


def extended(x, edge):
    lane = iota(edge.shape, edge.ndim - 1)
    last = jnp.where(
        lane < 104, x[..., 2 * TILE :], jnp.where(lane < 112, lane_roll(edge, 104), lane_roll(edge, 24))
    )
    return jnp.concatenate([x[..., : 2 * TILE], last], axis=-1)


def kernel(
    nx, ny, nlat, off_hbm, cos_hbm, x_hbm, w_hbm, pk_hbm, obs_hbm, ex_hbm, pg_ref, wb_ref,
    off_ref, cos_ref, x_raw, w_ref, pk_ref, obs_ref, ex_ref, in_sem, x_par, x_pad, obs_tmp, prod, qp, mask, csum, fsel, pgrad, su, sd, r_picks, zu, zd, r_sums,
    qpe, rqpe, own, yblk, xblk, fe, rfe, f0, f1, r_grad, f0e, f1e, r_rim, send_sem, recv_sem,
):
    ens = lax.axis_index("ens")
    lat = lax.axis_index("lat")
    lon = lax.axis_index("lon")
    ex, ey = ens // ny, ens % ny
    has_up = (lat + nlat - 1) // nlat
    has_down = (2 * nlat - 2 - lat) // nlat
    partner = 1 - lon
    have_up = has_up.astype(F32)
    have_down = has_down.astype(F32)
    up = {"t": lat - has_up, "n": has_up * lon + (1 - has_up) * partner}
    down = {"t": lat + has_down, "n": has_down * lon + (1 - has_down) * partner}
    up_partner = {"t": lat - has_up, "n": partner}
    down_partner = {"t": lat + has_down, "n": partner}

    def x_peer(d):
        return ((ex + d) % nx) * ny + ey

    def y_peer(d):
        return ex * ny + (ey + d) % ny

    def target(e=None, t=None, n=None):
        return (ens if e is None else e, lat if t is None else t, lon if n is None else n)

    def step_of(a, q):
        return off_ref[q, a].astype(F32)

    sems = [0]

    def remote(src, dst, device):
        i = sems[0]
        sems[0] += 1
        return pltpu.make_async_remote_copy(
            src_ref=src, dst_ref=dst, send_sem=send_sem.at[i], recv_sem=recv_sem.at[i],
            device_id=device, device_id_type=MESH,
        )

    barrier = pltpu.get_barrier_semaphore()
    peers = [target(n=partner)]
    peers += [target(**where) for where in (up, down, up_partner, down_partner)]
    peers += [target(e=x_peer(d)) for d in range(1, nx)] + [target(e=y_peer(d)) for d in range(1, ny)]
    for device in peers:
        pl.semaphore_signal(barrier, inc=1, device_id=device, device_id_type=MESH)

    inputs = {}
    pairs = [
        ("ex", ex_hbm, ex_ref), ("pk", pk_hbm, pk_ref), ("off", off_hbm, off_ref), ("x", x_hbm, x_raw),
        ("w", w_hbm, w_ref), ("obs", obs_hbm, obs_ref), ("cos", cos_hbm, cos_ref),
    ]
    for i, (name, src, dst) in enumerate(pairs):
        inputs[name] = pltpu.make_async_copy(src, dst, in_sem.at[i])
        inputs[name].start()

    pick = iota((256, 256), 0) - 2 * iota((256, 256), 1)
    half = iota((256, 256), 1)
    select = jnp.where((pick == jnp.where(half < TILE, 0, -255)), 1.0, 0.0).astype(BF16)
    columns = pk_ref.shape[2]
    widths = [slice(256 * block, min(256 * block + 256, columns)) for block in range(3)]
    inputs["ex"].wait()
    inputs["pk"].wait()
    picks = pk_ref[...].astype(F32).reshape(18, columns).astype(BF16)
    rows = jnp.dot(ex_ref[...], picks, preferred_element_type=F32).astype(BF16)
    inputs["off"].wait()
    row8 = iota((8, TILE), 0)
    for block in range(3):
        wide = widths[block]
        part = select[: wide.stop - wide.start]
        tile = slice(TILE * block, TILE * block + TILE)
        got = jnp.dot(rows[:, wide], part, preferred_element_type=F32)
        for slot in range(6):
            qp[0, slot, :, tile] = got[8 * slot : 8 * slot + 8, :TILE]
            qp[1, slot, :, tile] = got[8 * slot : 8 * slot + 8, TILE:]
        su[:, tile] = jnp.where(row8 == 6, step_of(0, 0), got[48:56, :TILE] + got[64:72, TILE:])
        sd[:, tile] = jnp.where(row8 == 6, step_of(2, 1), got[56:64, :TILE] + got[72:80, TILE:])
    pl.semaphore_wait(barrier, len(peers))
    started = []

    def go(src, dst, device):
        copy = remote(src, dst, device)
        copy.start()
        started.append(copy)
        return copy

    def halo(to_up, to_down, into, where_up, where_down):
        base = sems[0]
        sems[0] += 2
        slots = [(to_up, where_up, has_up), (to_down, where_down, 1 - has_down)]
        arrivals = []
        for i, (src, where, slot) in enumerate(slots):
            def copy(index, src=src, where=where, i=i):
                return pltpu.make_async_remote_copy(
                    src_ref=src, dst_ref=into.at[index], send_sem=send_sem.at[base + i],
                    recv_sem=recv_sem.at[base + index], device_id=target(**where), device_id_type=MESH,
                )

            out = copy(slot)
            out.start()
            started.append(out)
            arrivals.append(copy(i))
        return arrivals

    c_picks = halo(su, sd, r_picks, up, down)
    inputs["x"].wait()
    c_x = go(x_raw, x_par, target(n=partner))

    inputs["w"].wait()
    latents = 2 * x_raw.shape[0]
    one = jnp.where(iota((ROWS, 10), 0) // 2 == iota((ROWS, 10), 1), 1.0, 0.0).astype(BF16)
    spread = [jnp.dot(one, w_ref[k], preferred_element_type=F32) for k in range(BASES)]
    spread = jnp.concatenate(spread, axis=0).astype(BF16)
    shape = (w_ref.shape[2], latents)
    s2 = jnp.where(iota(shape, 1) // 2 == iota(shape, 0), 1.0, 0.0).astype(BF16)
    wf = jnp.dot(spread, s2, preferred_element_type=F32)
    wf = jnp.where(iota(wf.shape, 0) % 2 == iota(wf.shape, 1) % 2, wf, 0.0).astype(BF16)
    s2t = jnp.where(iota(shape[::-1], 0) // 2 == iota(shape[::-1], 1), 1.0, 0.0).astype(BF16)
    wb = lax.dot_general(s2t, spread, (((1,), (1,)), ((), ())), preferred_element_type=F32)
    wb_ref[...] = jnp.where(iota(wb.shape, 0) % 2 == iota(wb.shape, 1) % 2, wb, 0.0).astype(BF16)

    inputs["obs"].wait()
    obs = obs_ref[...].reshape(20, columns)
    obs_hi = obs.astype(BF16)
    obs_lo = (obs - obs_hi.astype(F32)).astype(BF16)
    obs_tmp[...] = jnp.zeros_like(obs_tmp)
    for block in range(3):
        wide = widths[block]
        part = select[: wide.stop - wide.start]
        tile = slice(TILE * block, TILE * block + TILE)
        both = jnp.dot(obs_hi[:, wide], part, preferred_element_type=F32) + jnp.dot(
            obs_lo[:, wide], part, preferred_element_type=F32
        )
        obs_tmp[: obs.shape[0], tile] = both[:, :TILE]
        obs_tmp[ROWS : ROWS + obs.shape[0], tile] = both[:, TILE:]
    inputs["cos"].wait()

    c_x.wait_recv()
    sector = []
    for i, raw in enumerate((x_raw, x_par)):
        x_pad[i, :, 2 * TILE :] = jnp.zeros((latents, TILE), BF16)
        x_pad[i, :, : columns // 2] = raw[...].reshape(latents, columns // 2)
        sector.append(x_pad[i].astype(F32))
    latent = extended(sector[0], edge_of(sector[1]))
    halfway = 0.5 * (latent + lane_roll(latent, -1))
    for parity, x in enumerate((latent, halfway)):
        got = jnp.dot(wf, x.astype(BF16), preferred_element_type=F32)
        prod[parity] = got.reshape(BASES, 3, 8, LANES)

    even = iota((8, LANES), 0) % 2 == 0
    even3 = iota((3, 8, LANES), 1) % 2 == 0
    steps = [
        jnp.where(even, step_of(1, 0), step_of(1, 1)),
        jnp.where(even, step_of(0, 1), step_of(2, 0)),
        None,
    ]

    def build_masks(kind, source):
        for b in (-1, 0, 1):
            slot = 3 * kind + b + 1
            pair = source(slot)
            if b:
                pair = shifted(pair, -b, steps[kind])
            for parity in (0, 1):
                mask[parity, slot] = pair[parity]

    def own_columns(slot):
        return [qp[0, slot], qp[1, slot]]

    def all_columns(slot):
        return [extended(qp[parity, slot], rqpe[parity, slot]) for parity in (0, 1)]

    def pick_products(slots):
        for parity in (0, 1):
            for t in range(3):
                tile = slice(TILE * t, TILE * t + TILE)
                values = [prod[parity, k, :, :, tile] for k in range(BASES)]
                for slot in slots:
                    want = jnp.broadcast_to(mask[parity, slot, :, tile][None], (3, 8, TILE))
                    total = jnp.where(want == 0.0, values[0], 0.0)
                    for k in range(1, BASES):
                        total = jnp.where(want == float(k), values[k], total)
                    csum[parity, slot, :, :, tile] = total

    def target_sum(kind):
        total = [csum[0, 3 * kind + 1], csum[1, 3 * kind + 1]]
        for b in (-1, 1):
            slot = 3 * kind + b + 1
            moved = shifted([csum[0, slot], csum[1, slot]], b, steps[kind])
            total = [x + y for x, y in zip(total, moved)]
        return total

    for kind in (0, 1):
        build_masks(kind, own_columns)
    pick_products(range(6))
    local = [x + swapped(y) for x, y in zip(target_sum(0), target_sum(1))]

    for copy in c_picks:
        copy.wait_recv()

    def spread_row(i):
        return jnp.where(
            even,
            jnp.broadcast_to(r_picks[0, i : i + 1, :], (8, LANES)),
            jnp.broadcast_to(r_picks[1, i : i + 1, :], (8, LANES)),
        )

    steps[2] = spread_row(6)
    for parity in (0, 1):
        for i in range(3):
            qp[parity, 6 + i] = spread_row(3 * parity + i)
    build_masks(2, own_columns)
    pick_products(range(6, 9))
    away = target_sum(2)
    zu[...] = jnp.where(even3, away[0], row_down(away[1])).reshape(ROWS, LANES).astype(zu.dtype)
    zd[...] = jnp.where(even3, row_up(away[0]), away[1]).reshape(ROWS, LANES).astype(zd.dtype)
    c_sums = halo(zu, zd, r_sums, up, down)
    for parity in (0, 1):
        qpe[parity] = edge_of(qp[parity])
    c_q = go(qpe, rqpe, target(n=partner))
    for copy in c_sums:
        copy.wait_recv()
    from_up = r_sums[0].astype(F32).reshape(3, 8, LANES) * have_up
    from_down = r_sums[1].astype(F32).reshape(3, 8, LANES) * have_down
    pred = [
        local[0] + jnp.where(even3, from_up, row_down(from_down)),
        local[1] + jnp.where(even3, row_up(from_up), from_down),
    ]
    mine = packed(pred)
    own[...] = mine.reshape(40, LANES).astype(BF16)

    def terms(ref):
        return smoothed_derivative(mine - ref[...].astype(F32).reshape(5, 8, LANES))

    def spread_along(block, slots, peer, relay):
        copies = [go(block, slots[0], peer(1)), go(block, slots[1], peer(-1))]
        if not relay and len(slots) > 2:
            copies.append(go(block, slots[2], peer(2)))
        return copies

    def pass_on(slots, peer, relay, copies):
        for i in (0, 1):
            copies[i].wait_recv()
            if relay:
                half = pl.ds(0, 24) if i == 0 else pl.ds(24, 16)
                copies.append(go(slots[i].at[half], slots[2].at[half], peer(1 if i == 0 else -1)))

    if nx == 4:
        def x_to(d):
            return target(e=x_peer(d % nx))

        def y_to(d):
            return target(e=y_peer(d % ny))

        y_slots = [yblk.at[i] for i in range(3)]
        x_slots = [[xblk.at[j, i] for i in range(3)] for j in range(4)]
        c_y = spread_along(own, y_slots, y_to, Y_RELAY)
        c_xs = [spread_along(own, x_slots[0], x_to, 0 in X_RELAY)]
        c_q.wait_recv()
        for kind in range(3):
            build_masks(kind, all_columns)
        pass_on(x_slots[0], x_to, 0 in X_RELAY, c_xs[0])
        pass_on(y_slots, y_to, Y_RELAY, c_y)
        for j in (1, 2):
            c_xs.append(spread_along(y_slots[j - 1], x_slots[j], x_to, j in X_RELAY))
        for copy in c_y[2:]:
            copy.wait_recv()
        c_xs.append(spread_along(y_slots[2], x_slots[3], x_to, 3 in X_RELAY))
        pair_total = terms(x_slots[0][0]) + terms(x_slots[0][1])
        for j in (1, 2, 3):
            pass_on(x_slots[j], x_to, j in X_RELAY, c_xs[j])
            pair_total += terms(y_slots[j - 1]) + terms(x_slots[j][0]) + terms(x_slots[j][1])
        for j in range(4):
            for copy in c_xs[j][2:]:
                copy.wait_recv()
            pair_total += terms(x_slots[j][2])
    else:
        c_y = [go(own, yblk.at[d - 1], target(e=y_peer(d))) for d in range(1, ny)]
        relayed = [[go(own, xblk.at[0, d - 1], target(e=x_peer(d))) for d in range(1, nx)]]
        pair_total = jnp.zeros_like(mine)
        for d in range(1, ny):
            c_y[d - 1].wait_recv()
            relayed.append([go(yblk.at[d - 1], xblk.at[d, e - 1], target(e=x_peer(e))) for e in range(1, nx)])
            pair_total += terms(yblk.at[d - 1])
        c_q.wait_recv()
        for kind in range(3):
            build_masks(kind, all_columns)
        for d in range(ny):
            for e in range(1, nx):
                relayed[d][e - 1].wait_recv()
                pair_total += terms(xblk.at[d, e - 1])
    pair_total = unpacked(pair_total)

    factor = jnp.where(even3, cos_ref[0], cos_ref[1])
    grad = []
    for parity in (0, 1):
        miss = pred[parity] - obs_tmp[ROWS * parity : ROWS * (parity + 1)].reshape(3, 8, LANES)
        grad.append(factor * (smoothed_derivative(miss) - pair_total[parity] * (1.0 / (nx * ny - 1))))
        fe[parity] = edge_of(grad[parity])
    lower = jnp.where(even3, grad[0], row_down(grad[1]))
    upper = jnp.where(even3, row_up(grad[0]), grad[1])
    f0[...] = lower.reshape(ROWS, LANES).astype(f0.dtype)
    f1[...] = upper.reshape(ROWS, LANES).astype(f1.dtype)
    f0e[...] = edge_of(lower).reshape(ROWS, TILE).astype(f0e.dtype)
    f1e[...] = edge_of(upper).reshape(ROWS, TILE).astype(f1e.dtype)
    c_fe = go(fe, rfe, target(n=partner))
    c_f = halo(f0, f1, r_grad, up, down) + halo(f0e, f1e, r_rim, up_partner, down_partner)

    def spread_gradient(kind, wide):
        for b in (-1, 0, 1):
            pair = shifted(wide, -b, steps[kind]) if b else wide
            for parity in (0, 1):
                fsel[parity, 3 * kind + b + 1] = pair[parity]

    def add_gradient(slots, first):
        for parity in (0, 1):
            for t in range(3):
                tile = slice(TILE * t, TILE * t + TILE)
                values = [fsel[parity, slot, :, :, tile] for slot in slots]
                wants = [jnp.broadcast_to(mask[parity, slot, :, tile][None], (3, 8, TILE)) for slot in slots]
                for k in range(BASES):
                    chosen = [jnp.where(want == float(k), value, 0.0) for want, value in zip(wants, values)]
                    if not first:
                        chosen.append(pgrad[parity, k, :, :, tile])
                    while len(chosen) > 1:
                        chosen = [x + y for x, y in zip(chosen[::2], chosen[1::2])] + chosen[len(chosen) & ~1 :]
                    pgrad[parity, k, :, :, tile] = chosen[0]

    c_fe.wait_recv()
    wide = [extended(grad[parity], rfe[parity]) for parity in (0, 1)]
    spread_gradient(0, wide)
    spread_gradient(1, [swapped(x) for x in wide])
    add_gradient(range(6), True)

    def neighbours(below, above):
        below = below.astype(F32).reshape(3, 8, -1) * have_down
        above = above.astype(F32).reshape(3, 8, -1) * have_up
        is_even = iota(below.shape, 1) % 2 == 0
        return [jnp.where(is_even, above, row_down(below)), jnp.where(is_even, row_up(above), below)]

    for copy in c_f:
        copy.wait_recv()
    inner, rim = neighbours(r_grad[1], r_grad[0]), neighbours(r_rim[1], r_rim[0])
    spread_gradient(2, [extended(x, edge) for x, edge in zip(inner, rim)])
    add_gradient(range(6, 9), False)

    odd = pgrad[1].reshape(BASES * ROWS, LANES)
    folded = pgrad[0].reshape(BASES * ROWS, LANES) + 0.5 * (odd + lane_roll(odd, 1))
    pg_ref[...] = folded.astype(BF16)

    for copy in started:
        copy.wait_send()


def last_product(wb_ref, pg_ref, out_ref):
    got = jnp.dot(wb_ref[...], pg_ref[...], preferred_element_type=F32)
    out_ref[...] = got[:, : out_ref.shape[2]].reshape(out_ref.shape)


def on_device(sizes, hidden_state, filter_coefficients, meridian_offset_table, function_pick_table, observation, latitude_cosine_factor):
    nx, ny, nlat = sizes
    channels, band, columns = hidden_state.shape[1:]
    hbm = pl.BlockSpec(memory_space=pltpu.HBM)
    vmem = pl.BlockSpec(memory_space=pltpu.VMEM)
    row = pltpu.VMEM((8, LANES), F32)
    sums = pltpu.VMEM((ROWS, LANES), SUMS)
    field = pltpu.VMEM((ROWS, LANES), HALO)
    edge = pltpu.VMEM((ROWS, TILE), HALO)
    raw = pltpu.VMEM((channels, band, columns), BF16)
    copies = 11 + 2 * (ny - 1) + 2 * ny * (nx - 1)
    gradient, weights = pl.pallas_call(
        functools.partial(kernel, nx, ny, nlat),
        out_shape=(
            jax.ShapeDtypeStruct((BASES * ROWS, LANES), BF16),
            jax.ShapeDtypeStruct((2 * channels, BASES * ROWS), BF16),
        ),
        in_specs=[hbm] * 7,
        out_specs=(vmem, vmem),
        scratch_shapes=[
            pltpu.SMEM((band, 3), jnp.int32),
            pltpu.SMEM((band,), F32),
            raw,
            pltpu.VMEM(filter_coefficients.shape, BF16),
            pltpu.VMEM(function_pick_table.shape, jnp.int32),
            pltpu.VMEM(observation.shape, F32),
            pltpu.VMEM((80, 18), BF16),
            pltpu.SemaphoreType.DMA((7,)),
            raw,
            pltpu.VMEM((2, 2 * channels, LANES), BF16),
            pltpu.VMEM((2 * ROWS, LANES), F32),
            pltpu.VMEM((2, 9, 3, 8, LANES), F32),
            pltpu.VMEM((2, 9, 8, LANES), F32),
            pltpu.VMEM((2, 9, 8, LANES), F32),
            pltpu.VMEM((2, 9, 3, 8, LANES), F32),
            pltpu.VMEM((2, 9, 3, 8, LANES), F32),
            pltpu.VMEM((2, 9, 3, 8, LANES), F32),
            row, row, pltpu.VMEM((2, 8, LANES), F32),
            sums, sums, pltpu.VMEM((2, ROWS, LANES), SUMS),
            pltpu.VMEM((2, 9, 8, TILE), F32),
            pltpu.VMEM((2, 9, 8, TILE), F32),
            pltpu.VMEM((40, LANES), BF16),
            pltpu.VMEM((ny - 1, 40, LANES), BF16),
            pltpu.VMEM((ny, nx - 1, 40, LANES), BF16),
            pltpu.VMEM((2, 3, 8, TILE), F32),
            pltpu.VMEM((2, 3, 8, TILE), F32),
            field, field, pltpu.VMEM((2, ROWS, LANES), HALO),
            edge, edge, pltpu.VMEM((2, ROWS, TILE), HALO),
            pltpu.SemaphoreType.DMA((copies,)),
            pltpu.SemaphoreType.DMA((copies,)),
        ],
        compiler_params=pltpu.CompilerParams(collective_id=0, has_side_effects=True, vmem_limit_bytes=16 << 20),
    )(
        *[
            pltpu.with_memory_space_constraint(array, pltpu.HBM)
            for array in (
                meridian_offset_table.T,
                latitude_cosine_factor,
                hidden_state.reshape(channels, band, columns),
                filter_coefficients,
                function_pick_table,
                observation,
                jnp.asarray(expand_picks(), BF16),
            )
        ]
    )
    out = pl.pallas_call(
        last_product,
        out_shape=jax.ShapeDtypeStruct((channels, band, columns), F32),
        in_specs=[vmem, vmem],
        out_specs=vmem,
        compiler_params=pltpu.CompilerParams(vmem_limit_bytes=16 << 20),
    )(weights, gradient)
    return out[None]


def solution(mesh):
    members = mesh.shape["ens"]
    nx = 4 if members % 4 == 0 and members > 4 else 2
    return jax.shard_map(
        functools.partial(on_device, (nx, members // nx, mesh.shape["lat"])),
        mesh=mesh,
        in_specs=(
            P("ens", None, "lat", "lon"),
            P(),
            P(None, "lat"),
            P(None, "lat", "lon"),
            P(None, "lat", "lon"),
            P("lat"),
        ),
        out_specs=P("ens", None, "lat", "lon"),
        check_vma=False,
    )
```

time: 48.2 us -> 37.9 us (0.79)
  the two profiles are of different devices: /device:TPU:1 before, /device:TPU:9 now
where the time goes in v2:
time: 37.9 us; the launch traced here: 37.7 us
  Pallas kernels  37.7 us (99%)
    pallas_call x1, Pallas kernels, on_device(): pl.pallas_call(functools.partial(kernel, nx, ny, nlat), out_shape=(jax.Sh...  36.8 us
    pallas_call x1, Pallas kernels, on_device(): pl.pallas_call(last_product, out_shape=jax.ShapeDtypeStruct((channels, ba...  0.91 us

profile of v2, /device:TPU:9, one launch (start us, length us, event | category | flops | bytes accessed | tf_op | source)
XLA Modules:
  0.0 37.7 jit_solution(11947168667594870059)
XLA Ops:
  0.0 36.8 %shard_map.73 = (bf16[216,384]{1,0:T(8,128)(2,1)S(1)}, bf16[180,216]{1,0:T(8,128)(2,1)S(1)}) custom-call(s32[2,3]{1,0:T(2,128)} %bitcast.4, f32[2]{0:T(128)} %cos_hbm.1, bf16[90,2,360]{2,1,0:T(2,128)(2,1)} %bitcast.3, bf16[9,10,90]{2,1,0:T(8,128)(2,1)} %w_hbm.1, s32[9,2,720]{2,1,0:T(2,128)} %pk_hbm.1, f32[10,2,720]{2,1,0:T(2,128)} %obs_hbm.1, ...), custom_call_target="tpu_custom_call" | custom-call | tf_op jit(solution)/shard_map/pallas_call | solution.py:477
  36.8 0.9 %shard_map.74 = f32[90,2,360]{2,1,0:T(2,128)} custom-call(bf16[180,216]{1,0:T(8,128)(2,1)S(1)} %get-tuple-element.7.wb_ref, bf16[216,384]{1,0:T(8,128)(2,1)S(1)} %get-tuple-element.8.pg_ref), custom_call_target="tpu_custom_call" | custom-call | tf_op jit(solution)/shard_map/pallas_call | solution.py:532

commit v3 on v2

--- a/solution.py
+++ b/solution.py
@@ -18,21 +18,22 @@
 BF16 = jnp.bfloat16
 MESH = pl.DeviceIdType.MESH
 HALO = BF16
-SUMS = F32
-Y_RELAY = False
-X_RELAY = ()
+DEEP = 96
+PIECES = ((0, 40),)
+ALONG_Y = (1, -1, 2)
 
 
 def expand_picks():
-    rows = np.zeros((80, 18), np.float32)
+    rows = np.zeros((104, 18), np.float32)
     for i in range(3):
         for sub in range(8):
             rows[8 * i + sub, 2 * (3 + i) + (sub & 1)] = 1
             rows[24 + 8 * i + sub, 2 * (6 + i) if sub & 1 else 2 * i + 1] = 1
-        rows[48 + i, 2 * i] = 1
-        rows[56 + i, 2 * (6 + i) + 1] = 1
-        rows[64 + 3 + i, 2 * i] = 1
-        rows[72 + 3 + i, 2 * (6 + i) + 1] = 1
+            rows[48 + 8 * i + sub, 2 * (6 + i) + 1 if sub & 1 else 2 * i] = 1
+        rows[72 + i, 2 * i] = 1
+        rows[80 + i, 2 * (6 + i) + 1] = 1
+        rows[88 + 3 + i, 2 * i] = 1
+        rows[96 + 3 + i, 2 * (6 + i) + 1] = 1
     return rows
 
 
@@ -105,7 +106,8 @@
 
 def kernel(
     nx, ny, nlat, off_hbm, cos_hbm, x_hbm, w_hbm, pk_hbm, obs_hbm, ex_hbm, pg_ref, wb_ref,
-    off_ref, cos_ref, x_raw, w_ref, pk_ref, obs_ref, ex_ref, in_sem, x_par, x_pad, obs_tmp, prod, qp, mask, csum, fsel, pgrad, su, sd, r_picks, zu, zd, r_sums,
+    off_ref, cos_ref, x_raw, w_ref, pk_ref, obs_ref, ex_ref, in_sem, x_par, x_pad, x_row, x_rim, r_row, r_edge, obs_tmp,
+    prod, far, qpf, qp, mask, csum, fsel, pgrad, su, sd, r_picks,
     qpe, rqpe, own, yblk, xblk, fe, rfe, f0, f1, r_grad, f0e, f1e, r_rim, send_sem, recv_sem,
 ):
     ens = lax.axis_index("ens")
@@ -159,6 +161,42 @@
     for i, (name, src, dst) in enumerate(pairs):
         inputs[name] = pltpu.make_async_copy(src, dst, in_sem.at[i])
         inputs[name].start()
+
+    inputs["x"].wait()
+    x_row[...] = jnp.zeros_like(x_row)
+    for r in (0, 1):
+        x_row[r, : x_raw.shape[0], : x_raw.shape[2]] = x_raw[:, r, :]
+        x_rim[r] = edge_of(x_row[r].astype(F32)).astype(BF16)
+    pl.semaphore_wait(barrier, len(peers))
+    started = []
+
+    def go(src, dst, device):
+        copy = remote(src, dst, device)
+        copy.start()
+        started.append(copy)
+        return copy
+
+    def halo(to_up, to_down, into, where_up, where_down):
+        base = sems[0]
+        sems[0] += 2
+        slots = [(to_up, where_up, has_up), (to_down, where_down, 1 - has_down)]
+        arrivals = []
+        for i, (src, where, slot) in enumerate(slots):
+            def copy(index, src=src, where=where, i=i):
+                return pltpu.make_async_remote_copy(
+                    src_ref=src, dst_ref=into.at[index], send_sem=send_sem.at[base + i],
+                    recv_sem=recv_sem.at[base + index], device_id=target(**where), device_id_type=MESH,
+                )
+
+            out = copy(slot)
+            out.start()
+            started.append(out)
+            arrivals.append(copy(i))
+        return arrivals
+
+    c_rows = halo(x_row.at[0], x_row.at[1], r_row, up, down)
+    c_rims = halo(x_rim.at[0], x_rim.at[1], r_edge, up_partner, down_partner)
+    c_x = go(x_raw, x_par, target(n=partner))
 
     pick = iota((256, 256), 0) - 2 * iota((256, 256), 1)
     half = iota((256, 256), 1)
@@ -179,38 +217,12 @@
         for slot in range(6):
             qp[0, slot, :, tile] = got[8 * slot : 8 * slot + 8, :TILE]
             qp[1, slot, :, tile] = got[8 * slot : 8 * slot + 8, TILE:]
-        su[:, tile] = jnp.where(row8 == 6, step_of(0, 0), got[48:56, :TILE] + got[64:72, TILE:])
-        sd[:, tile] = jnp.where(row8 == 6, step_of(2, 1), got[56:64, :TILE] + got[72:80, TILE:])
-    pl.semaphore_wait(barrier, len(peers))
-    started = []
-
-    def go(src, dst, device):
-        copy = remote(src, dst, device)
-        copy.start()
-        started.append(copy)
-        return copy
-
-    def halo(to_up, to_down, into, where_up, where_down):
-        base = sems[0]
-        sems[0] += 2
-        slots = [(to_up, where_up, has_up), (to_down, where_down, 1 - has_down)]
-        arrivals = []
-        for i, (src, where, slot) in enumerate(slots):
-            def copy(index, src=src, where=where, i=i):
-                return pltpu.make_async_remote_copy(
-                    src_ref=src, dst_ref=into.at[index], send_sem=send_sem.at[base + i],
-                    recv_sem=recv_sem.at[base + index], device_id=target(**where), device_id_type=MESH,
-                )
-
-            out = copy(slot)
-            out.start()
-            started.append(out)
-            arrivals.append(copy(i))
-        return arrivals
-
+        for slot in range(3):
+            qpf[0, slot, :, tile] = got[48 + 8 * slot : 56 + 8 * slot, :TILE]
+            qpf[1, slot, :, tile] = got[48 + 8 * slot : 56 + 8 * slot, TILE:]
+        su[:, tile] = jnp.where(row8 == 6, step_of(0, 0), got[72:80, :TILE] + got[88:96, TILE:])
+        sd[:, tile] = jnp.where(row8 == 6, step_of(2, 1), got[80:88, :TILE] + got[96:104, TILE:])
     c_picks = halo(su, sd, r_picks, up, down)
-    inputs["x"].wait()
-    c_x = go(x_raw, x_par, target(n=partner))
 
     inputs["w"].wait()
     latents = 2 * x_raw.shape[0]
@@ -224,6 +236,10 @@
     s2t = jnp.where(iota(shape[::-1], 0) // 2 == iota(shape[::-1], 1), 1.0, 0.0).astype(BF16)
     wb = lax.dot_general(s2t, spread, (((1,), (1,)), ((), ())), preferred_element_type=F32)
     wb_ref[...] = jnp.where(iota(wb.shape, 0) % 2 == iota(wb.shape, 1) % 2, wb, 0.0).astype(BF16)
+    shape = (w_ref.shape[2], 2 * DEEP)
+    s3 = jnp.where(iota(shape, 1) % DEEP == iota(shape, 0), 1.0, 0.0).astype(BF16)
+    wn = jnp.dot(spread, s3, preferred_element_type=F32)
+    wn = jnp.where((iota(wn.shape, 0) % 2 == 0) == (iota(wn.shape, 1) < DEEP), wn, 0.0).astype(BF16)
 
     inputs["obs"].wait()
     obs = obs_ref[...].reshape(20, columns)
@@ -258,7 +274,7 @@
     steps = [
         jnp.where(even, step_of(1, 0), step_of(1, 1)),
         jnp.where(even, step_of(0, 1), step_of(2, 0)),
-        None,
+        jnp.where(even, step_of(0, 0), step_of(2, 1)),
     ]
 
     def build_masks(kind, source):
@@ -276,11 +292,11 @@
     def all_columns(slot):
         return [extended(qp[parity, slot], rqpe[parity, slot]) for parity in (0, 1)]
 
-    def pick_products(slots):
+    def pick_products(product, slots):
         for parity in (0, 1):
             for t in range(3):
                 tile = slice(TILE * t, TILE * t + TILE)
-                values = [prod[parity, k, :, :, tile] for k in range(BASES)]
+                values = [product[parity, k, :, :, tile] for k in range(BASES)]
                 for slot in slots:
                     want = jnp.broadcast_to(mask[parity, slot, :, tile][None], (3, 8, TILE))
                     total = jnp.where(want == 0.0, values[0], 0.0)
@@ -298,11 +314,22 @@
 
     for kind in (0, 1):
         build_masks(kind, own_columns)
-    pick_products(range(6))
+    pick_products(prod, range(6))
     local = [x + swapped(y) for x, y in zip(target_sum(0), target_sum(1))]
-
-    for copy in c_picks:
+    build_masks(2, lambda slot: [qpf[0, slot - 6], qpf[1, slot - 6]])
+
+    for copy in c_rows + c_rims:
         copy.wait_recv()
+    around_x = extended(
+        r_row[...].reshape(2 * DEEP, LANES).astype(F32), r_edge[...].reshape(2 * DEEP, TILE).astype(F32)
+    )
+    for parity, x in enumerate((around_x, 0.5 * (around_x + lane_roll(around_x, -1)))):
+        far[parity] = jnp.dot(wn, x.astype(BF16), preferred_element_type=F32).reshape(BASES, 3, 8, LANES)
+    pick_products(far, range(6, 9))
+    present = jnp.where(even3, have_up, have_down)
+    pred = [x + present * y for x, y in zip(local, target_sum(2))]
+    mine = packed(pred)
+    own[...] = mine.reshape(40, LANES).astype(BF16)
 
     def spread_row(i):
         return jnp.where(
@@ -311,75 +338,49 @@
             jnp.broadcast_to(r_picks[1, i : i + 1, :], (8, LANES)),
         )
 
-    steps[2] = spread_row(6)
-    for parity in (0, 1):
-        for i in range(3):
-            qp[parity, 6 + i] = spread_row(3 * parity + i)
-    build_masks(2, own_columns)
-    pick_products(range(6, 9))
-    away = target_sum(2)
-    zu[...] = jnp.where(even3, away[0], row_down(away[1])).reshape(ROWS, LANES).astype(zu.dtype)
-    zd[...] = jnp.where(even3, row_up(away[0]), away[1]).reshape(ROWS, LANES).astype(zd.dtype)
-    c_sums = halo(zu, zd, r_sums, up, down)
-    for parity in (0, 1):
-        qpe[parity] = edge_of(qp[parity])
-    c_q = go(qpe, rqpe, target(n=partner))
-    for copy in c_sums:
-        copy.wait_recv()
-    from_up = r_sums[0].astype(F32).reshape(3, 8, LANES) * have_up
-    from_down = r_sums[1].astype(F32).reshape(3, 8, LANES) * have_down
-    pred = [
-        local[0] + jnp.where(even3, from_up, row_down(from_down)),
-        local[1] + jnp.where(even3, row_up(from_up), from_down),
-    ]
-    mine = packed(pred)
-    own[...] = mine.reshape(40, LANES).astype(BF16)
+    def backward_masks():
+        for copy in c_picks:
+            copy.wait_recv()
+        steps[2] = spread_row(6)
+        for parity in (0, 1):
+            for i in range(3):
+                qp[parity, 6 + i] = spread_row(3 * parity + i)
+            qpe[parity] = edge_of(qp[parity])
+        go(qpe, rqpe, target(n=partner)).wait_recv()
+        for kind in range(3):
+            build_masks(kind, all_columns)
 
     def terms(ref):
         return smoothed_derivative(mine - ref[...].astype(F32).reshape(5, 8, LANES))
 
-    def spread_along(block, slots, peer, relay):
-        copies = [go(block, slots[0], peer(1)), go(block, slots[1], peer(-1))]
-        if not relay and len(slots) > 2:
-            copies.append(go(block, slots[2], peer(2)))
-        return copies
-
-    def pass_on(slots, peer, relay, copies):
-        for i in (0, 1):
-            copies[i].wait_recv()
-            if relay:
-                half = pl.ds(0, 24) if i == 0 else pl.ds(24, 16)
-                copies.append(go(slots[i].at[half], slots[2].at[half], peer(1 if i == 0 else -1)))
-
     if nx == 4:
-        def x_to(d):
-            return target(e=x_peer(d % nx))
-
-        def y_to(d):
-            return target(e=y_peer(d % ny))
-
-        y_slots = [yblk.at[i] for i in range(3)]
-        x_slots = [[xblk.at[j, i] for i in range(3)] for j in range(4)]
-        c_y = spread_along(own, y_slots, y_to, Y_RELAY)
-        c_xs = [spread_along(own, x_slots[0], x_to, 0 in X_RELAY)]
-        c_q.wait_recv()
-        for kind in range(3):
-            build_masks(kind, all_columns)
-        pass_on(x_slots[0], x_to, 0 in X_RELAY, c_xs[0])
-        pass_on(y_slots, y_to, Y_RELAY, c_y)
-        for j in (1, 2):
-            c_xs.append(spread_along(y_slots[j - 1], x_slots[j], x_to, j in X_RELAY))
-        for copy in c_y[2:]:
-            copy.wait_recv()
-        c_xs.append(spread_along(y_slots[2], x_slots[3], x_to, 3 in X_RELAY))
-        pair_total = terms(x_slots[0][0]) + terms(x_slots[0][1])
-        for j in (1, 2, 3):
-            pass_on(x_slots[j], x_to, j in X_RELAY, c_xs[j])
-            pair_total += terms(y_slots[j - 1]) + terms(x_slots[j][0]) + terms(x_slots[j][1])
-        for j in range(4):
-            for copy in c_xs[j][2:]:
-                copy.wait_recv()
-            pair_total += terms(x_slots[j][2])
+        ring = (1, -1, 2)
+
+        def slot(dx, dy, rows):
+            place = xblk.at[ring.index(dy) + 1 if dy else 0, ring.index(dx)] if dx else yblk.at[ring.index(dy)]
+            return place.at[pl.ds(*rows)]
+
+        arrivals = {}
+        for rows in PIECES:
+            for dy in ALONG_Y:
+                arrivals[0, dy, rows] = go(own.at[pl.ds(*rows)], slot(0, dy, rows), target(e=y_peer(dy % ny)))
+        for rows in PIECES:
+            for dx in ring:
+                arrivals[dx, 0, rows] = go(own.at[pl.ds(*rows)], slot(dx, 0, rows), target(e=x_peer(dx % nx)))
+        backward_masks()
+        for rows in PIECES:
+            for dy in ring:
+                arrivals[0, dy, rows].wait_recv()
+                for dx in ring:
+                    arrivals[dx, dy, rows] = go(slot(0, dy, rows), slot(dx, dy, rows), target(e=x_peer(dx % nx)))
+        pair_total = jnp.zeros_like(mine)
+        for dy in (0, *ring):
+            if dy:
+                pair_total += terms(yblk.at[ring.index(dy)])
+            for dx in ring:
+                for rows in PIECES:
+                    arrivals[dx, dy, rows].wait_recv()
+                pair_total += terms(xblk.at[ring.index(dy) + 1 if dy else 0, ring.index(dx)])
     else:
         c_y = [go(own, yblk.at[d - 1], target(e=y_peer(d))) for d in range(1, ny)]
         relayed = [[go(own, xblk.at[0, d - 1], target(e=x_peer(d))) for d in range(1, nx)]]
@@ -388,9 +389,7 @@
             c_y[d - 1].wait_recv()
             relayed.append([go(yblk.at[d - 1], xblk.at[d, e - 1], target(e=x_peer(e))) for e in range(1, nx)])
             pair_total += terms(yblk.at[d - 1])
-        c_q.wait_recv()
-        for kind in range(3):
-            build_masks(kind, all_columns)
+        backward_masks()
         for d in range(ny):
             for e in range(1, nx):
                 relayed[d][e - 1].wait_recv()
@@ -469,7 +468,6 @@
     hbm = pl.BlockSpec(memory_space=pltpu.HBM)
     vmem = pl.BlockSpec(memory_space=pltpu.VMEM)
     row = pltpu.VMEM((8, LANES), F32)
-    sums = pltpu.VMEM((ROWS, LANES), SUMS)
     field = pltpu.VMEM((ROWS, LANES), HALO)
     edge = pltpu.VMEM((ROWS, TILE), HALO)
     raw = pltpu.VMEM((channels, band, columns), BF16)
@@ -489,19 +487,24 @@
             pltpu.VMEM(filter_coefficients.shape, BF16),
             pltpu.VMEM(function_pick_table.shape, jnp.int32),
             pltpu.VMEM(observation.shape, F32),
-            pltpu.VMEM((80, 18), BF16),
+            pltpu.VMEM((104, 18), BF16),
             pltpu.SemaphoreType.DMA((7,)),
             raw,
             pltpu.VMEM((2, 2 * channels, LANES), BF16),
+            pltpu.VMEM((2, DEEP, LANES), BF16),
+            pltpu.VMEM((2, DEEP, TILE), BF16),
+            pltpu.VMEM((2, DEEP, LANES), BF16),
+            pltpu.VMEM((2, DEEP, TILE), BF16),
             pltpu.VMEM((2 * ROWS, LANES), F32),
             pltpu.VMEM((2, 9, 3, 8, LANES), F32),
+            pltpu.VMEM((2, 9, 3, 8, LANES), F32),
+            pltpu.VMEM((2, 3, 8, LANES), F32),
             pltpu.VMEM((2, 9, 8, LANES), F32),
             pltpu.VMEM((2, 9, 8, LANES), F32),
             pltpu.VMEM((2, 9, 3, 8, LANES), F32),
             pltpu.VMEM((2, 9, 3, 8, LANES), F32),
             pltpu.VMEM((2, 9, 3, 8, LANES), F32),
             row, row, pltpu.VMEM((2, 8, LANES), F32),
-            sums, sums, pltpu.VMEM((2, ROWS, LANES), SUMS),
             pltpu.VMEM((2, 9, 8, TILE), F32),
             pltpu.VMEM((2, 9, 8, TILE), F32),
             pltpu.VMEM((40, LANES), BF16),

time: 37.9 us -> 35.5 us (0.937)
  Pallas kernels: 37.7 us -> 35.3 us
    pallas_call x1, Pallas kernels: 36.8 us -> 34.4 us  [on_device(): pl.pallas_call(functools.partial(kernel, nx, ny, nlat), out_shape=(jax.Sh...]
where the time goes in v3:
time: 35.5 us; the launch traced here: 35.3 us
  Pallas kernels  35.3 us (99%)
    pallas_call x1, Pallas kernels, on_device(): pl.pallas_call(functools.partial(kernel, nx, ny, nlat), out_shape=(jax.Sh...  34.4 us
    pallas_call x1, Pallas kernels, on_device(): pl.pallas_call(last_product, out_shape=jax.ShapeDtypeStruct((channels, ba...  0.92 us

profile of v3, /device:TPU:9, one launch (start us, length us, event | category | flops | bytes accessed | tf_op | source)
XLA Modules:
  0.0 35.3 jit_solution(10260430717558838657)
XLA Ops:
  0.0 34.4 %shard_map.73 = (bf16[216,384]{1,0:T(8,128)(2,1)S(1)}, bf16[180,216]{1,0:T(8,128)(2,1)S(1)}) custom-call(s32[2,3]{1,0:T(2,128)} %bitcast.4, f32[2]{0:T(128)} %cos_hbm.1, bf16[90,2,360]{2,1,0:T(2,128)(2,1)} %bitcast.3, bf16[9,10,90]{2,1,0:T(8,128)(2,1)} %w_hbm.1, s32[9,2,720]{2,1,0:T(2,128)} %pk_hbm.1, f32[10,2,720]{2,1,0:T(2,128)} %obs_hbm.1, ...), custom_call_target="tpu_custom_call" | custom-call | tf_op jit(solution)/shard_map/pallas_call | solution.py:475
  34.4 0.9 %shard_map.74 = f32[90,2,360]{2,1,0:T(2,128)} custom-call(bf16[180,216]{1,0:T(8,128)(2,1)S(1)} %get-tuple-element.7.wb_ref, bf16[216,384]{1,0:T(8,128)(2,1)S(1)} %get-tuple-element.8.pg_ref), custom_call_target="tpu_custom_call" | custom-call | tf_op jit(solution)/shard_map/pallas_call | solution.py:535

commit v4 on v3

--- a/solution.py
+++ b/solution.py
@@ -108,7 +108,7 @@
     nx, ny, nlat, off_hbm, cos_hbm, x_hbm, w_hbm, pk_hbm, obs_hbm, ex_hbm, pg_ref, wb_ref,
     off_ref, cos_ref, x_raw, w_ref, pk_ref, obs_ref, ex_ref, in_sem, x_par, x_pad, x_row, x_rim, r_row, r_edge, obs_tmp,
     prod, far, qpf, qp, mask, csum, fsel, pgrad, su, sd, r_picks,
-    qpe, rqpe, own, yblk, xblk, fe, rfe, f0, f1, r_grad, f0e, f1e, r_rim, send_sem, recv_sem,
+    qpe, rqpe, own, yblk, xblk, fe, rfe, f0, f1, r_grad, f0e, f1e, r_rim, ring_sem, send_sem, recv_sem,
 ):
     ens = lax.axis_index("ens")
     lat = lax.axis_index("lat")
@@ -146,27 +146,36 @@
             device_id=device, device_id_type=MESH,
         )
 
-    barrier = pltpu.get_barrier_semaphore()
-    peers = [target(n=partner)]
-    peers += [target(**where) for where in (up, down, up_partner, down_partner)]
-    peers += [target(e=x_peer(d)) for d in range(1, nx)] + [target(e=y_peer(d)) for d in range(1, ny)]
-    for device in peers:
-        pl.semaphore_signal(barrier, inc=1, device_id=device, device_id_type=MESH)
-
     inputs = {}
     pairs = [
-        ("ex", ex_hbm, ex_ref), ("pk", pk_hbm, pk_ref), ("off", off_hbm, off_ref), ("x", x_hbm, x_raw),
+        ("x", x_hbm, x_raw), ("ex", ex_hbm, ex_ref), ("pk", pk_hbm, pk_ref), ("off", off_hbm, off_ref),
         ("w", w_hbm, w_ref), ("obs", obs_hbm, obs_ref), ("cos", cos_hbm, cos_ref),
     ]
     for i, (name, src, dst) in enumerate(pairs):
         inputs[name] = pltpu.make_async_copy(src, dst, in_sem.at[i])
         inputs[name].start()
 
+    barrier = pltpu.get_barrier_semaphore()
+    peers = [target(n=partner)]
+    peers += [target(**where) for where in (up, down, up_partner, down_partner)]
+    peers += [target(e=x_peer(d)) for d in (1, nx - 1)[: nx - 1]] + [target(e=y_peer(d)) for d in (1, ny - 1)[: ny - 1]]
+    for device in peers:
+        pl.semaphore_signal(barrier, inc=1, device_id=device, device_id_type=MESH)
+
+    channels, latent_columns = x_raw.shape[0], x_raw.shape[2]
+    latents = 2 * channels
+    shape = (2 * DEEP, latents)
+    wanted = jnp.where(iota(shape, 0) < DEEP, 2 * iota(shape, 0), 2 * (iota(shape, 0) - DEEP) + 1)
+    wanted = jnp.where(wanted == iota(shape, 1), 1.0, 0.0).astype(BF16)
+    for i in (0, 1):
+        x_pad[i, :, 2 * TILE :] = jnp.zeros((latents, TILE), BF16)
     inputs["x"].wait()
-    x_row[...] = jnp.zeros_like(x_row)
+    x_pad[0, :, :latent_columns] = x_raw[...].reshape(latents, latent_columns)
+    split = jnp.dot(wanted, x_pad[0], preferred_element_type=F32)
     for r in (0, 1):
-        x_row[r, : x_raw.shape[0], : x_raw.shape[2]] = x_raw[:, r, :]
-        x_rim[r] = edge_of(x_row[r].astype(F32)).astype(BF16)
+        row = split[DEEP * r : DEEP * (r + 1)]
+        x_row[r] = row.astype(BF16)
+        x_rim[r] = edge_of(row).astype(BF16)
     pl.semaphore_wait(barrier, len(peers))
     started = []
 
@@ -194,6 +203,9 @@
             arrivals.append(copy(i))
         return arrivals
 
+    if nx == 4:
+        for device in (target(e=x_peer(1)), target(e=y_peer(1))):
+            pl.semaphore_signal(ring_sem, inc=1, device_id=device, device_id_type=MESH)
     c_rows = halo(x_row.at[0], x_row.at[1], r_row, up, down)
     c_rims = halo(x_rim.at[0], x_rim.at[1], r_edge, up_partner, down_partner)
     c_x = go(x_raw, x_par, target(n=partner))
@@ -225,7 +237,6 @@
     c_picks = halo(su, sd, r_picks, up, down)
 
     inputs["w"].wait()
-    latents = 2 * x_raw.shape[0]
     one = jnp.where(iota((ROWS, 10), 0) // 2 == iota((ROWS, 10), 1), 1.0, 0.0).astype(BF16)
     spread = [jnp.dot(one, w_ref[k], preferred_element_type=F32) for k in range(BASES)]
     spread = jnp.concatenate(spread, axis=0).astype(BF16)
@@ -258,11 +269,8 @@
     inputs["cos"].wait()
 
     c_x.wait_recv()
-    sector = []
-    for i, raw in enumerate((x_raw, x_par)):
-        x_pad[i, :, 2 * TILE :] = jnp.zeros((latents, TILE), BF16)
-        x_pad[i, :, : columns // 2] = raw[...].reshape(latents, columns // 2)
-        sector.append(x_pad[i].astype(F32))
+    x_pad[1, :, :latent_columns] = x_par[...].reshape(latents, latent_columns)
+    sector = [x_pad[i].astype(F32) for i in (0, 1)]
     latent = extended(sector[0], edge_of(sector[1]))
     halfway = 0.5 * (latent + lane_roll(latent, -1))
     for parity, x in enumerate((latent, halfway)):
@@ -360,6 +368,7 @@
             place = xblk.at[ring.index(dy) + 1 if dy else 0, ring.index(dx)] if dx else yblk.at[ring.index(dy)]
             return place.at[pl.ds(*rows)]
 
+        pl.semaphore_wait(ring_sem, 2)
         arrivals = {}
         for rows in PIECES:
             for dy in ALONG_Y:
@@ -514,6 +523,7 @@
             pltpu.VMEM((2, 3, 8, TILE), F32),
             field, field, pltpu.VMEM((2, ROWS, LANES), HALO),
             edge, edge, pltpu.VMEM((2, ROWS, TILE), HALO),
+            pltpu.SemaphoreType.REGULAR,
             pltpu.SemaphoreType.DMA((copies,)),
             pltpu.SemaphoreType.DMA((copies,)),
         ],

time: 35.5 us -> 35.3 us (level)
  no operation moved by 1% of the time
where the time goes in v4:
time: 35.3 us; the launch traced here: 35.2 us
  Pallas kernels  35.2 us (100%)
    pallas_call x1, Pallas kernels, on_device(): pl.pallas_call(functools.partial(kernel, nx, ny, nlat), out_shape=(jax.Sh...  34.3 us
    pallas_call x1, Pallas kernels, on_device(): pl.pallas_call(last_product, out_shape=jax.ShapeDtypeStruct((channels, ba...  0.91 us

profile of v4, /device:TPU:9, one launch (start us, length us, event | category | flops | bytes accessed | tf_op | source)
XLA Modules:
  0.0 35.2 jit_solution(3586825139131543808)
XLA Ops:
  0.0 34.3 %shard_map.73 = (bf16[216,384]{1,0:T(8,128)(2,1)S(1)}, bf16[180,216]{1,0:T(8,128)(2,1)S(1)}) custom-call(s32[2,3]{1,0:T(2,128)} %bitcast.4, f32[2]{0:T(128)} %cos_hbm.1, bf16[90,2,360]{2,1,0:T(2,128)(2,1)} %bitcast.3, bf16[9,10,90]{2,1,0:T(8,128)(2,1)} %w_hbm.1, s32[9,2,720]{2,1,0:T(2,128)} %pk_hbm.1, f32[10,2,720]{2,1,0:T(2,128)} %obs_hbm.1, ...), custom_call_target="tpu_custom_call" | custom-call | tf_op jit(solution)/shard_map/pallas_call | solution.py:484
  34.3 0.9 %shard_map.74 = f32[90,2,360]{2,1,0:T(2,128)} custom-call(bf16[180,216]{1,0:T(8,128)(2,1)S(1)} %get-tuple-element.7.wb_ref, bf16[216,384]{1,0:T(8,128)(2,1)S(1)} %get-tuple-element.8.pg_ref), custom_call_target="tpu_custom_call" | custom-call | tf_op jit(solution)/shard_map/pallas_call | solution.py:545

commit v5 on v4

--- a/solution.py
+++ b/solution.py
@@ -206,8 +206,8 @@
     if nx == 4:
         for device in (target(e=x_peer(1)), target(e=y_peer(1))):
             pl.semaphore_signal(ring_sem, inc=1, device_id=device, device_id_type=MESH)
+    c_rims = halo(x_rim.at[0], x_rim.at[1], r_edge, up_partner, down_partner)
     c_rows = halo(x_row.at[0], x_row.at[1], r_row, up, down)
-    c_rims = halo(x_rim.at[0], x_rim.at[1], r_edge, up_partner, down_partner)
     c_x = go(x_raw, x_par, target(n=partner))
 
     pick = iota((256, 256), 0) - 2 * iota((256, 256), 1)
@@ -380,7 +380,7 @@
         for rows in PIECES:
             for dy in ring:
                 arrivals[0, dy, rows].wait_recv()
-                for dx in ring:
+                for dx in (2, 1, -1):
                     arrivals[dx, dy, rows] = go(slot(0, dy, rows), slot(dx, dy, rows), target(e=x_peer(dx % nx)))
         pair_total = jnp.zeros_like(mine)
         for dy in (0, *ring):

time: 35.3 us -> 35.1 us (level)
  no operation moved by 1% of the time
where the time goes in v5:
time: 35.1 us; the launch traced here: 35 us
  Pallas kernels  34.9 us (99%)
    pallas_call x1, Pallas kernels, on_device(): pl.pallas_call(functools.partial(kernel, nx, ny, nlat), out_shape=(jax.Sh...  34 us
    pallas_call x1, Pallas kernels, on_device(): pl.pallas_call(last_product, out_shape=jax.ShapeDtypeStruct((channels, ba...  0.91 us

profile of v5, /device:TPU:9, one launch (start us, length us, event | category | flops | bytes accessed | tf_op | source)
XLA Modules:
  0.0 35.0 jit_solution(17594850811976301216)
XLA Ops:
  0.0 34.0 %shard_map.73 = (bf16[216,384]{1,0:T(8,128)(2,1)S(1)}, bf16[180,216]{1,0:T(8,128)(2,1)S(1)}) custom-call(s32[2,3]{1,0:T(2,128)} %bitcast.4, f32[2]{0:T(128)} %cos_hbm.1, bf16[90,2,360]{2,1,0:T(2,128)(2,1)} %bitcast.3, bf16[9,10,90]{2,1,0:T(8,128)(2,1)} %w_hbm.1, s32[9,2,720]{2,1,0:T(2,128)} %pk_hbm.1, f32[10,2,720]{2,1,0:T(2,128)} %obs_hbm.1, ...), custom_call_target="tpu_custom_call" | custom-call | tf_op jit(solution)/shard_map/pallas_call | solution.py:484
  34.0 0.9 %shard_map.74 = f32[90,2,360]{2,1,0:T(2,128)} custom-call(bf16[180,216]{1,0:T(8,128)(2,1)S(1)} %get-tuple-element.7.wb_ref, bf16[216,384]{1,0:T(8,128)(2,1)S(1)} %get-tuple-element.8.pg_ref), custom_call_target="tpu_custom_call" | custom-call | tf_op jit(solution)/shard_map/pallas_call | solution.py:545
